TPU v7x, 32 devices: a whole 2x2x4 slice. The times are simulated.
32 devices in a mesh: mem: 4 (over z), state: 8 (over y, x, core).
Axes of the slice: x: 2, y: 2, z: 4, core: 2. Of those that a mesh axis runs over, the one named last changes fastest.
Arguments:
- anomalies: bfloat16 [64, 32, 32768], P('mem', None, 'state'), may hold values from -0.75 to 0.75
- alpha: bfloat16 [64, 32, 2048], P('mem', None, 'state'), may hold values from -6 to 6
- basis: bfloat16 [2048, 32768], P(None, 'state'), may hold values from -0.1875 to 0.1875
- gradient: bfloat16 [32, 32768], P(None, 'state'), may hold values from -6 to 6
- vertical_root: float32 [32, 32], replicated, may hold values from -1 to 1
- band_gain: float32 [16], replicated, may hold values from 0.25 to 2
- band: int32 [2048], P('state'), may hold values from 0 to 15
- order: int32 [64], replicated, may hold values from 0 to 63, each once
Outputs:
- increment: float32 [32, 32768], P(None, 'state')
- alpha_grad: float32 [64, 32, 2048], P('mem', None, 'state')
Inputs may be any that keep to these rules, and one draw needn't show every extreme that they name: `order`: a permutation: every member is named by exactly one slot.
All inputs are finite; a program needn't handle non-finite values.
Results may differ from a plain program's by a relative error of at most 0.0029.
Values may be sent and summed in bfloat16 or wider, within the bound.
A program may use at most 128 MiB of HBM per device.

v0:
```python
import functools
import jax
import jax.numpy as jnp
from jax import lax
from jax.experimental import pallas as pl
from jax.experimental.pallas import tpu as pltpu
from jax.sharding import PartitionSpec as P

MESH = pl.DeviceIdType.MESH
F32 = jnp.float32
BF16 = jnp.bfloat16
NT = (((1,), (1,)), ((), ()))


def flip(a, k, n):
    out, bit = 0, 1
    while bit < n:
        out = out + lax.rem(lax.div(a, bit) + (k // bit) % 2, 2) * bit
        bit *= 2
    return out


def kernel(
    zn, sn, levels,
    table, gain, vroot, alpha, gradient, anomalies, basis,
    inc_out, grad_out,
    anom, base, weighted, coef_all, mine, pair_out, pair_in, rs_out, rs_in,
    pick_all, grad_all, acc, inc_own, inc_stage, inc_in, inc_red, pack, got,
    anom_sem, base_sem, z_send, z_recv, pair_send, pair_recv, rs_send, rs_recv,
    pk_send, pk_recv, fw_send, fw_recv, g_send, g_recv, is_send, is_recv, ia_send, ia_recv,
):
    z = lax.axis_index("mem")
    s = lax.axis_index("state")
    chip, core = lax.div(s, 2), lax.rem(s, 2)
    qn = sn // 2
    partner = chip * 2 + (1 - core)
    rows, cols = alpha.shape
    columns = anom.shape[1]
    members = rows // levels
    high = lax.Precision.HIGHEST

    zpeer = [flip(z, k, zn) for k in range(zn)]
    qpeer = [flip(chip, k, qn) for k in range(qn)]

    def load_of(t, n):
        return pltpu.make_async_copy(basis.at[t], base.at[t], base_sem.at[n])

    order_of_q = list(range(qn - 1, -1, -1))
    anom_copy = pltpu.make_async_copy(anomalies, anom, anom_sem)
    anom_copy.start()
    loads = []
    for i, k in enumerate(order_of_q):
        loads.append((load_of(qpeer[k] * 2 + 1 - core, 2 * i), load_of(qpeer[k] * 2 + core, 2 * i + 1)))
        loads[-1][0].start()
        loads[-1][1].start()

    barrier = pltpu.get_barrier_semaphore()
    for k in range(1, zn):
        pl.semaphore_signal(barrier, inc=1, device_id={"mem": zpeer[k]}, device_id_type=MESH)
    for k in range(1, qn):
        pl.semaphore_signal(barrier, inc=1, device_id={"state": qpeer[k] * 2 + core}, device_id_type=MESH)
    pl.semaphore_signal(barrier, inc=1, device_id={"state": partner}, device_id_type=MESH)

    def to(src, dst, send, recv, **where):
        return pltpu.make_async_remote_copy(
            src_ref=src, dst_ref=dst, send_sem=send, recv_sem=recv, device_id=where, device_id_type=MESH
        )

    own_rows = pl.ds(z * members, members)
    line = zn == 4
    outer = lax.div(lax.rem(z + 1, zn), 2) == 0
    inner = jnp.logical_not(outer)

    class Exchange:
        def __init__(self, row, held, mine, packed, send, recv):
            self.row, self.held, self.mine, self.packed = row, held, mine, packed
            own = held.at[own_rows]
            if not line:
                self.copies = [
                    to(own, own, send.at[k], recv.at[k], mem=zpeer[k]) for k in range(1, zn)
                ]
                return
            self.near = 1 + lax.rem(z, 2)
            self.far = lax.max(z - 1, 0) * 3 - lax.max(z - 2, 0) * 3
            rim = held.at[pl.ds(self.far * members, members)]
            kind = lax.rem(lax.div(z + 1, 2), 2)
            self.first = to(own, own, send.at[0], recv.at[kind], mem=self.near)
            self.from_rim = to(own, own, send.at[0], recv.at[0], mem=self.near)
            self.from_inner = to(own, own, send.at[0], recv.at[1], mem=self.near)
            self.relay = to(rim, rim, send.at[1], recv.at[2], mem=self.near)
            self.give = to(packed, mine, send.at[2], recv.at[3], mem=self.far)

        def start(self):
            for copy in [self.first] if line else self.copies:
                copy.start()

        def pass_on(self):
            if line:

                @pl.when(inner)
                def _():
                    self.from_rim.wait_recv()
                    self.relay.start()

        def pick(self, out, who):
            for m in range(members):
                out[pl.ds(m * levels, levels), :] = self.held[table[self.row, who * members + m]]

        def finish(self):
            if not line:
                for copy in self.copies:
                    copy.wait_recv()
                self.pick(self.mine, z)
                return

            @pl.when(inner)
            def _():
                self.from_inner.wait_recv()
                self.relay.wait_recv()
                self.pick(self.packed, self.far)
                self.give.start()
                self.pick(self.mine, z)

        def settle(self):
            if line:

                @pl.when(outer)
                def _():
                    self.give.wait_recv()

        def drain(self):
            if not line:
                for copy in self.copies:
                    copy.wait_send()
                return
            self.first.wait_send()

            @pl.when(inner)
            def _():
                self.relay.wait_send()
                self.give.wait_send()

    row_of = lax.broadcasted_iota(jnp.int32, (rows, levels), 0)
    level_of = lax.broadcasted_iota(jnp.int32, (rows, levels), 1)
    expand = jnp.where(lax.rem(row_of, levels) == level_of, 1.0, 0.0).astype(F32)
    here_of = lax.broadcasted_iota(jnp.int32, (rows, rows), 0)
    there_of = lax.broadcasted_iota(jnp.int32, (rows, rows), 1)
    same = lax.div(here_of, levels) == lax.div(there_of, levels)

    def blocks(tall):
        full = lax.dot_general(tall, expand, NT, precision=high, preferred_element_type=F32)
        return jnp.where(same, full, 0.0)

    root = blocks(jnp.dot(expand, vroot[...], precision=high, preferred_element_type=F32))
    coef = jnp.dot(root, alpha[...].astype(F32), precision=high, preferred_element_type=F32)
    coef_all[own_rows] = (coef * gain[...]).astype(BF16).reshape(members, levels, -1)
    pl.semaphore_wait(barrier, zn - 1 + qn)
    coef_ex = Exchange(0, coef_all, pick_all.at[s], pack.at[0], z_send, z_recv)
    coef_ex.start()

    anom_copy.wait()

    def weigh(m, carry):
        at = pl.ds(pl.multiple_of(m * levels, levels), levels)
        weighted[at, :] = (anom[at, :].astype(F32) * gradient[...].astype(F32)).astype(BF16)
        return carry

    lax.fori_loop(0, members, weigh, 0)

    pairs = [
        to(pair_out.at[i], pair_in.at[i], pair_send.at[i], pair_recv.at[i], state=partner) for i in range(qn)
    ]
    scatters = [
        to(rs_out.at[i], rs_in.at[i], rs_send.at[i], rs_recv.at[i], state=qpeer[k] * 2 + core)
        for i, k in enumerate(order_of_q[:-1])
    ]

    half = rows // 2

    def project(t, store):
        def part(h, carry):
            at = pl.ds(pl.multiple_of(h * half, half), half)
            store(at, lax.dot_general(weighted[at, :], base[t], NT, preferred_element_type=F32))
            return carry

        lax.fori_loop(0, 2, part, 0)

    def combine(i):
        pairs[i].wait_recv()
        total = mine[i] + pair_in[i]
        if i < qn - 1:
            rs_out[i] = total.astype(BF16)
            scatters[i].start()
        else:
            mine[i] = total

    for i, k in enumerate(order_of_q):
        loads[i][0].wait()

        def put_pair(at, v, i=i):
            pair_out[i, at, :] = v

        def put_mine(at, v, i=i):
            mine[i, at, :] = v

        project(qpeer[k] * 2 + 1 - core, put_pair)
        pairs[i].start()
        if i > 0:
            combine(i - 1)
        loads[i][1].wait()
        project(qpeer[k] * 2 + core, put_mine)
        if i == qn // 2 - 1:
            coef_ex.pass_on()

    coef_ex.finish()
    combine(qn - 1)
    coef_ex.settle()
    picks = [to(pick_all.at[s], pick_all.at[s], pk_send.at[0], pk_recv.at[0], state=partner)] + [
        to(pick_all.at[s], pick_all.at[s], pk_send.at[k], pk_recv.at[k], state=qpeer[k] * 2 + core)
        for k in range(1, qn)
    ]
    for copy in picks:
        copy.start()

    pieces = zn
    width = columns // pieces

    def spread(t, first):
        def part(j, carry):
            at = pl.ds(pl.multiple_of(j * width, width), width)
            field = jnp.dot(pick_all[t], base[t, :, at], preferred_element_type=F32)
            acc[:, at] = field if first else acc[:, at] + field
            return carry

        lax.fori_loop(0, pieces, part, 0)

    spread(s, True)
    for copy in scatters:
        copy.wait_recv()
    total = mine[qn - 1]
    for i in range(qn - 1):
        total = total + rs_in[i].astype(F32)
    root_t = blocks(lax.dot_general(expand, vroot[...], NT, precision=high, preferred_element_type=F32))
    grad = jnp.dot(root_t, total, precision=high, preferred_element_type=F32)
    grad_all[own_rows] = (grad * gain[...]).astype(BF16).reshape(members, levels, -1)
    grad_ex = Exchange(1, grad_all, got, pack.at[1], g_send, g_recv)
    grad_ex.start()
    picks[0].wait_recv()
    spread(partner, False)

    forwards = [None]
    for k in range(1, qn):
        t, o = qpeer[k] * 2 + core, qpeer[k] * 2 + 1 - core
        picks[k].wait_recv()
        forwards.append(to(pick_all.at[t], pick_all.at[t], fw_send.at[k], fw_recv.at[k], state=partner))
        forwards[k].start()
        spread(t, False)
        forwards[k].wait_recv()
        if k < qn - 1:
            spread(o, False)
        if k == qn // 2:
            grad_ex.pass_on()

    last = qpeer[qn - 1] * 2 + 1 - core
    sums = [None] + [
        to(inc_stage.at[k], inc_in.at[k], is_send.at[k], is_recv.at[k], mem=zpeer[k]) for k in range(1, zn)
    ]
    for k in list(range(1, zn)) + [0]:
        at = pl.ds(pl.multiple_of(zpeer[k] * width, width), width)

        def one(m, run, at=at):
            here = pl.ds(pl.multiple_of(m * 4 * levels, 4 * levels), 4 * levels)
            field = acc[here, at] + jnp.dot(pick_all[last, here, :], base[last, :, at], preferred_element_type=F32)
            prod = field * anom[here, at].astype(F32)
            for u in range(4):
                run = run + prod[u * levels : (u + 1) * levels]
            return run

        run = jnp.zeros((levels, width), F32)
        for m in range(members // 4):
            run = one(m, run)
        if k > 0:
            inc_stage[k] = run.astype(BF16)
            sums[k].start()
        else:
            inc_own[...] = run
    grad_ex.finish()
    run = inc_own[...]
    for k in range(1, zn):
        sums[k].wait_recv()
        run = run + inc_in[k].astype(F32)
    inc_red[z] = run.astype(BF16)
    shares = [
        to(inc_red.at[z], inc_red.at[z], ia_send.at[k], ia_recv.at[k], mem=zpeer[k]) for k in range(1, zn)
    ]
    for copy in shares:
        copy.start()

    grad_ex.settle()
    grad_out[...] = got[...]

    for copy in shares:
        copy.wait_recv()
    for b in range(zn):
        inc_out[:, b * width : (b + 1) * width] = inc_red[b]
    coef_ex.drain()
    grad_ex.drain()
    for copy in pairs + scatters + picks + forwards[1:] + sums[1:] + shares:
        copy.wait_send()


def on_device(zn, sn, anomalies, alpha, basis, gradient, vertical_root, band_gain, band, order):
    members, levels, columns = anomalies.shape
    mode_rows = alpha.shape[2]
    bands = band_gain.shape[0]
    rows = members * levels
    onehot = (band[:, None] == jnp.arange(bands, dtype=jnp.int32)[None, :]).astype(F32)
    gain = jnp.sum(onehot * band_gain[None, :], axis=1)[None, :]
    slots = jnp.arange(order.shape[0], dtype=jnp.int32)
    slot_of = jnp.sum(jnp.where(order[None, :] == slots[:, None], slots[None, :], 0), axis=1)
    table = jnp.stack([slot_of, order])
    qn = sn // 2
    width = columns // zn
    vmem = pl.BlockSpec(memory_space=pltpu.VMEM)
    hbm = pl.BlockSpec(memory_space=pl.ANY)
    dma = pltpu.SemaphoreType.DMA
    increment, grads = pl.pallas_call(
        functools.partial(kernel, zn, sn, levels),
        out_shape=(
            jax.ShapeDtypeStruct((levels, columns), BF16),
            jax.ShapeDtypeStruct((rows, mode_rows), BF16),
        ),
        in_specs=[pl.BlockSpec(memory_space=pltpu.SMEM)] + [vmem] * 4 + [hbm] * 2,
        out_specs=(vmem, vmem),
        scratch_shapes=[
            pltpu.VMEM((rows, columns), BF16),
            pltpu.VMEM((sn, mode_rows, columns), BF16),
            pltpu.VMEM((rows, columns), BF16),
            pltpu.VMEM((zn * members, levels, mode_rows), BF16),
            pltpu.VMEM((qn, rows, mode_rows), F32),
            pltpu.VMEM((qn, rows, mode_rows), F32),
            pltpu.VMEM((qn, rows, mode_rows), F32),
            pltpu.VMEM((qn, rows, mode_rows), BF16),
            pltpu.VMEM((qn, rows, mode_rows), BF16),
            pltpu.VMEM((sn, rows, mode_rows), BF16),
            pltpu.VMEM((zn * members, levels, mode_rows), BF16),
            pltpu.VMEM((rows, columns), F32),
            pltpu.VMEM((levels, width), F32),
            pltpu.VMEM((zn, levels, width), BF16),
            pltpu.VMEM((zn, levels, width), BF16),
            pltpu.VMEM((zn, levels, width), BF16),
            pltpu.VMEM((2, rows, mode_rows), BF16),
            pltpu.VMEM((rows, mode_rows), BF16),
            dma, dma((sn,)), dma((zn,)), dma((zn,)), dma((qn,)), dma((qn,)), dma((qn,)), dma((qn,)),
            dma((qn,)), dma((qn,)), dma((qn,)), dma((qn,)), dma((zn,)), dma((zn,)), dma((zn,)), dma((zn,)),
            dma((zn,)), dma((zn,)),
        ],
        compiler_params=pltpu.CompilerParams(
            collective_id=0, has_side_effects=True, vmem_limit_bytes=58 * 2**20
        ),
    )(
        table, gain, vertical_root, alpha.reshape(rows, mode_rows), gradient,
        anomalies.reshape(rows, columns), basis.reshape(sn, mode_rows, columns),
    )
    return increment.astype(F32), grads.astype(F32).reshape(members, levels, mode_rows)


def solution(mesh):
    zn, sn = mesh.shape["mem"], mesh.shape["state"]
    return jax.shard_map(
        functools.partial(on_device, zn, sn),
        mesh=mesh,
        in_specs=(
            P("mem", None, "state"),
            P("mem", None, "state"),
            P(None, "state"),
            P(None, "state"),
            P(),
            P(),
            P("state"),
            P(),
        ),
        out_specs=(P(None, "state"), P("mem", None, "state")),
        check_vma=False,
    )
```

profile of v0, /device:TPU:0, one launch (start us, length us, event | category | flops | bytes accessed | tf_op | source)
XLA Modules:
  0.0 69.7 jit_solution(1706499378336571084)
XLA Ops:
  0.6 0.8 %select_reduce_fusion = s32[64]{0:T(128)S(1)} fusion(s32[64]{0:T(128)} %param.15), kind=kLoop, calls=%fused_computation | loop fusion | flops 12224 | bytes 512 | tf_op jit(solution)/shard_map/reduce_sum | solution.py:320
  1.4 1.2 %pad_add_fusion.table = s32[2,64]{1,0:T(2,128)} fusion(s32[1,64]{1,0:T(1,128)} %bitcast.13, s32[1,64]{1,0:T(1,128)S(1)} %bitcast.14), kind=kLoop, calls=%fused_computation.4 | loop fusion | flops 128 | bytes 1024 | tf_op jit(solution)/shard_map/stack | solution.py:321
  2.6 1.3 %select_reduce_fusion.1 = f32[256]{0:T(256)} fusion(f32[16]{0:T(128)} %param.13, s32[256]{0:T(256)} %param.14), kind=kLoop, calls=%fused_computation.2 | loop fusion | flops 12032 | bytes 2112 | tf_op jit(solution)/shard_map/reduce_sum | solution.py:318
  4.0 62.2 %shard_map.95 = (bf16[32,4096]{1,0:T(8,128)(2,1)}, bf16[512,256]{1,0:T(8,128)(2,1)}) custom-call(s32[2,64]{1,0:T(2,128)} %pad_add_fusion.table, f32[1,256]{1,0:T(1,128)} %bitcast.12, f32[32,32]{1,0:T(8,128)} %vroot.1, bf16[512,256]{1,0:T(8,128)(2,1)} %bitcast.10, bf16[32,4096]{1,0:T(8,128)(2,1)} %gradient.1, bf16[512,4096]{1,0:T(8,128)(2,1)} %bitcast.9, ...), custom_call_target="tpu_custom_call" | custom-call | tf_op jit(solution)/shard_map/pallas_call | solution.py:327
  66.1 1.8 %convert.1 = f32[16,32,256]{2,1,0:T(8,128)} convert(bf16[16,32,256]{2,1,0:T(8,128)(2,1)} %bitcast.11) | non-fusion elementwise | flops 131072 | bytes 786432 | tf_op jit(solution)/shard_map/reshape | solution.py:365
  67.9 1.8 %convert_element_type.2 = f32[32,4096]{1,0:T(8,128)} convert(bf16[32,4096]{1,0:T(8,128)(2,1)} %get-tuple-element.4) | non-fusion elementwise | flops 131072 | bytes 786432 | tf_op jit(solution)/shard_map/convert_element_type | solution.py:365
where the time goes:
time: 69.9 us; the launch traced here: 69.7 us
  Pallas kernels  62.2 us (89%)
  other arithmetic  6.91 us (10%)
    pallas_call x1, Pallas kernels, on_device(): pl.pallas_call(functools.partial(kernel, zn, sn, levels), out_shape=(jax....  62.2 us
    reshape x1, other arithmetic, on_device(): grads.astype(F32).reshape(members, levels, mode_rows)  1.79 us
    convert_element_type x1, other arithmetic, on_device(): increment.astype(F32)  1.78 us

commit v1 on v0

v1 whole, which is shorter than its diff:
```python
import functools
import types
import jax
import jax.numpy as jnp
from jax import lax
from jax.experimental import pallas as pl
from jax.experimental.pallas import tpu as pltpu
from jax.sharding import PartitionSpec as P

MESH = pl.DeviceIdType.MESH
F32 = jnp.float32
BF16 = jnp.bfloat16
NT = (((1,), (1,)), ((), ()))
LANES = 128
GROUP = 256
HALVES = 2
STRIPS = 4


def flip(a, k, n):
    out, bit = 0, 1
    while bit < n:
        out = out + lax.rem(lax.div(a, bit) + (k // bit) % 2, 2) * bit
        bit *= 2
    return out


def split(v):
    high = v.astype(BF16)
    return high, (v - high.astype(F32)).astype(BF16)


def kernel(
    zn, sn, names,
    order, band_gain, vroot_h, alpha_h, band_h, gradient_h, anomalies, basis,
    inc_out, grad_out, *scratch,
):
    r = types.SimpleNamespace(**dict(zip(names, scratch)))
    coef_held = [ref for name, ref in zip(names, scratch) if name.startswith("coef_held")]
    grad_held = [ref for name, ref in zip(names, scratch) if name.startswith("grad_held")]
    z = lax.axis_index("mem")
    s = lax.axis_index("state")
    chip, core = lax.div(s, 2), lax.rem(s, 2)
    qn = sn // 2
    partner = chip * 2 + (1 - core)
    members, levels, columns = r.anom.shape
    modes = r.alpha.shape[1]
    parts = len(coef_held)
    _, lv, gw = coef_held[0].shape
    groups = modes // gw
    rows = members * levels
    slots = zn * members
    width = columns // STRIPS
    line, square = zn == 4, qn == 4

    zpeer = [flip(z, k, zn) for k in range(zn)]
    qpeer = [flip(chip, k, qn) for k in range(qn)]
    if square:
        first = qpeer[1] * (1 - core) + qpeer[2] * core
        second = qpeer[2] * (1 - core) + qpeer[1] * core
        chips = [qpeer[3], first, second, chip]
        chips_there = [qpeer[3], second, first, chip]
    else:
        chips = [qpeer[k] for k in range(qn - 1, -1, -1)]
        chips_there = chips

    barrier = pltpu.get_barrier_semaphore()
    for k in range(1, zn):
        pl.semaphore_signal(barrier, inc=1, device_id={"mem": zpeer[k]}, device_id_type=MESH)
    for k in range(1, qn):
        pl.semaphore_signal(barrier, inc=1, device_id={"state": qpeer[k] * 2 + core}, device_id_type=MESH)
    pl.semaphore_signal(barrier, inc=1, device_id={"state": partner}, device_id_type=MESH)

    small = [
        pltpu.make_async_copy(src, dst, r.load_sem.at[i])
        for i, (src, dst) in enumerate(
            [(vroot_h, r.vroot), (alpha_h, r.alpha), (band_h, r.band), (gradient_h, r.gradient), (anomalies, r.anom)]
        )
    ]
    for copy in small:
        copy.start()

    def load_of(g, t, n):
        here = pl.ds(g * gw, gw)
        return pltpu.make_async_copy(basis.at[t, here], r.base.at[t, here], r.base_sem.at[n])

    loads = []
    for g in range(groups):
        for i in range(qn):
            n = 2 * (g * qn + i)
            loads.append((load_of(g, chips_there[i] * 2 + 1 - core, n), load_of(g, chips[i] * 2 + core, n + 1)))
            loads[-1][0].start()
            loads[-1][1].start()

    def to(src, dst, send, recv, **where):
        return pltpu.make_async_remote_copy(
            src_ref=src, dst_ref=dst, send_sem=send, recv_sem=recv, device_id=where, device_id_type=MESH
        )

    spot = lax.broadcasted_iota(jnp.int32, r.inv_v.shape, 1)
    inverse = jnp.zeros(r.inv_v.shape, jnp.int32)
    for j in range(slots):
        inverse = jnp.where(spot == order[j], j, inverse)
    r.inv_v[...] = inverse
    inv_copy = pltpu.make_async_copy(r.inv_v, r.inv_s, r.inv_sem)
    inv_copy.start()

    own_rows = pl.ds(z * members, members)
    outer = lax.div(lax.rem(z + 1, zn), 2) == 0
    inner = jnp.logical_not(outer)
    near = 1 + lax.div(z, 2)
    mid = 3 - near
    other = 3 - z
    rim = (z - 1) * 3
    distant = 3 - rim

    class Exchange:
        def __init__(self, find, held, pack, mine, height, send, recv):
            self.find, self.held, self.pack, self.mine, self.height = find, held, pack, mine, height
            own = held.at[own_rows]
            if not line:
                self.out = [to(own, own, send.at[k], recv.at[z], mem=zpeer[k]) for k in range(1, zn)]
                self.come = [self.arrival(zpeer[k], send, recv, zpeer[k]) for k in range(1, zn)]
                return
            self.to_mid = to(own, own, send.at[0], recv.at[z], mem=mid)
            self.to_near = to(own, own, send.at[1], recv.at[z], mem=near)
            self.to_other = to(own, own, send.at[0], recv.at[z], mem=other)
            self.give = to(pack, mine, send.at[2], recv.at[z], mem=rim)
            self.given = to(pack, mine, send.at[2], recv.at[near], mem=near)
            self.come = [self.arrival(a, send, recv, other) for a in (rim, other, distant)]

        def arrival(self, a, send, recv, where):
            there = self.held.at[pl.ds(a * members, members)]
            return to(there, there, send.at[0], recv.at[a], mem=where)

        def start(self):
            if not line:
                for copy in self.out:
                    copy.start()
                return

            @pl.when(outer)
            def _():
                self.to_mid.start()
                self.to_near.start()

            @pl.when(inner)
            def _():
                self.to_other.start()

        def choose(self, out, who):
            for m in range(members):
                out[m * self.height : (m + 1) * self.height, :] = self.held[self.find(who * members + m)]

        def take_inner(self):
            for copy in self.come:
                copy.wait_recv()
            self.choose(self.pack, rim)
            self.give.start()
            self.choose(self.mine, z)

        def take_outer(self):
            self.given.wait_recv()

        def take(self):
            for copy in self.come:
                copy.wait_recv()
            self.choose(self.mine, z)

        def drain(self):
            if not line:
                for copy in self.out:
                    copy.wait_send()
                return

            @pl.when(outer)
            def _():
                self.to_mid.wait_send()
                self.to_near.wait_send()

            @pl.when(inner)
            def _():
                self.to_other.wait_send()
                self.give.wait_send()

    grid = (GROUP, levels)
    row_of = lax.broadcasted_iota(jnp.int32, grid, 0)
    level_of = lax.broadcasted_iota(jnp.int32, grid, 1)
    chunk = GROUP // HALVES
    piece_level = lax.div(row_of, chunk) * lv + lax.rem(row_of, lv)
    plain = jnp.where(lax.rem(row_of, levels) == level_of, 1.0, 0.0).astype(BF16)
    pieced = jnp.where(piece_level == level_of, 1.0, 0.0).astype(BF16)
    wide = (GROUP, GROUP)
    here_of = lax.broadcasted_iota(jnp.int32, wide, 0)
    there_of = lax.div(lax.broadcasted_iota(jnp.int32, wide, 1), levels)
    same_plain = lax.div(here_of, levels) == there_of
    same_pieced = lax.div(lax.rem(here_of, chunk), lv) == there_of

    def dot(a, b):
        return jnp.dot(a, b, preferred_element_type=F32)

    def dot_nt(a, b):
        return lax.dot_general(a, b, NT, preferred_element_type=F32)

    def blocks(tall, same):
        full = dot_nt(tall.astype(BF16), plain)
        return jnp.where(same, full, 0.0).astype(BF16)

    with jax.named_scope("coef"):
        small[0].wait()
        root_terms = split(r.vroot[...])
        root = [blocks(dot(pieced, v), same_pieced) for v in root_terms]
        root_t = [blocks(dot_nt(plain, v), same_plain) for v in root_terms]
        for v, keep in zip(root_t, (0, 1)):
            r.root_t[keep] = v
        small[1].wait()
        small[2].wait()
        band = r.band[...].reshape(1, modes)
        gain = jnp.zeros((1, modes), F32)
        for b in range(band_gain.shape[0]):
            gain = jnp.where(band == b, band_gain[b], gain)
        r.gain[...] = gain
        for n in range(rows // GROUP):
            control = r.alpha[n * GROUP : (n + 1) * GROUP, :]
            coef = (dot(root[0], control) + dot(root[1], control)) * gain
            coef = coef.astype(BF16)
            count = GROUP // levels
            for c in range(HALVES):
                for g in range(groups):
                    block = coef[c * chunk : (c + 1) * chunk, g * gw : (g + 1) * gw]
                    at = pl.ds(z * members + n * count, count)
                    coef_held[c * groups + g][at] = block.reshape(count, lv, gw)
    with jax.named_scope("barrier"):
        pl.semaphore_wait(barrier, zn - 1 + qn)

    coef_ex = [
        Exchange(
            lambda m: r.inv_s[0, m], coef_held[p], r.coef_pack.at[p], r.pick.at[p, s], lv,
            r.z_send.at[p], r.z_recv.at[p],
        )
        for p in range(parts)
    ]
    for ex in coef_ex:
        ex.start()
    grad_ex = [
        Exchange(
            lambda m: order[m], grad_held[g], r.grad_pack.at[g], r.got.at[g], levels,
            r.g_send.at[g], r.g_recv.at[g],
        )
        for g in range(groups)
    ]

    with jax.named_scope("weigh"):
        small[3].wait()
        small[4].wait()

        def weigh(m, carry):
            at = pl.ds(pl.multiple_of(m * levels, levels), levels)
            r.weighted[at, :] = (r.anom[m].astype(F32) * r.gradient[...].astype(F32)).astype(BF16)
            return carry

        lax.fori_loop(0, members, weigh, 0)

    def block_of(p, t):
        return r.pick.at[p, t]

    def share(p, t, i, where):
        return to(block_of(p, t), block_of(p, t), r.pk_send.at[p, i], r.pk_recv.at[p, t], state=where)

    class Gather:
        def __init__(self, p):
            self.p = p
            if square:
                self.out = [
                    share(p, s, 0, first * 2 + core), share(p, s, 1, second * 2 + core), share(p, s, 2, partner)
                ]
                tf, ts, td = first * 2 + core, second * 2 + core, qpeer[3] * 2 + core
                self.relay = share(p, tf, 3, second * 2 + core)
                self.arrive = [share(p, t, 4, partner) for t in (tf, ts, td)]
                self.over = [share(p, t, 4 + i, partner) for i, t in enumerate((tf, ts, td))]
            else:
                self.out = [share(p, s, k - 1, qpeer[k] * 2 + core) for k in range(1, qn)]
                self.out.append(share(p, s, qn - 1, partner))
                blocks_there = [qpeer[k] * 2 + core for k in range(1, qn)]
                self.arrive = [share(p, t, qn, partner) for t in blocks_there]
                self.over = [share(p, t, qn + i, partner) for i, t in enumerate(blocks_there)]
            self.rest = [share(p, qpeer[k] * 2 + 1 - core, 0, partner) for k in range(qn)]

        def start(self):
            for copy in self.out:
                copy.start()

        def pass_on(self):
            if square:
                self.arrive[0].wait_recv()
                self.relay.start()
                self.over[0].start()
                self.arrive[1].wait_recv()
                self.over[1].start()
            else:
                for come, go in zip(self.arrive, self.over):
                    come.wait_recv()
                    go.start()

        def pass_last(self):
            if square:
                self.arrive[2].wait_recv()
                self.over[2].start()

        def finish(self):
            for copy in self.rest:
                copy.wait_recv()

        def drain(self):
            for copy in self.out + self.over + ([self.relay] if square else []):
                copy.wait_send()

    gathers = [Gather(p) for p in range(parts)]

    def serve_inner(p):
        if line and p < parts:

            @pl.when(inner)
            def _():
                coef_ex[p].take_inner()
                gathers[p].start()

    def serve_outer(p):
        if line and p < parts:

            @pl.when(outer)
            def _():
                coef_ex[p].take_outer()
                gathers[p].start()

    def serve_all(p):
        if not line and p < parts:
            coef_ex[p].take()
            gathers[p].start()

    pairs = [
        to(r.pair_out.at[n], r.pair_in.at[n], r.pair_send.at[n], r.pair_recv.at[n], state=partner)
        for n in range(groups * qn)
    ]
    scatters = []
    for g in range(groups):
        if square:
            via = [(r.relay_in.at[g], first), (r.rs_in.at[g, 0], first), (r.rs_in.at[g, 1], second)]
        else:
            via = [(r.rs_in.at[g, i], chips[i]) for i in range(qn - 1)]
        scatters.append([
            to(r.rs_out.at[g, i], dst, r.rs_send.at[g, i], r.rs_recv.at[g, i], state=where * 2 + core)
            for i, (dst, where) in enumerate(via)
        ])

    def unit(g, i):
        n = g * qn + i
        for copy in loads[n]:
            copy.wait()
        cut = slice(g * gw, (g + 1) * gw)
        rhs = jnp.concatenate(
            [r.base[chips_there[i] * 2 + 1 - core, cut, :], r.base[chips[i] * 2 + core, cut, :]], axis=0
        )
        both = dot_nt(r.weighted[...], rhs)
        r.pair_out[n] = both[:, :gw]
        r.mine[n] = both[:, gw:]

    def combine(g, i):
        n = g * qn + i
        pairs[n].wait_recv()
        total = r.mine[n] + r.pair_in[n]
        if i == qn - 1:
            r.mine[n] = total
            return
        if square and i == 2:
            scatters[g][0].wait_recv()
            total = total + r.relay_in[g].astype(F32)
        r.rs_out[g, i] = total.astype(BF16)
        scatters[g][i].start()

    def adjoint(g):
        for copy in scatters[g][1:] if square else scatters[g]:
            copy.wait_recv()
        total = r.mine[g * qn + qn - 1]
        for i in range(r.rs_in.shape[1]):
            total = total + r.rs_in[g, i].astype(F32)
        stack = jnp.concatenate([total[n * GROUP : (n + 1) * GROUP] for n in range(rows // GROUP)], axis=1)
        high, low = split(stack)
        grad = dot(r.root_t[0], high) + dot(r.root_t[0], low) + dot(r.root_t[1], high)
        scale = r.gain[:, g * gw : (g + 1) * gw]
        count = GROUP // levels
        for n in range(rows // GROUP):
            block = (grad[:, n * gw : (n + 1) * gw] * scale).astype(BF16)
            grad_held[g][pl.ds(z * members + n * count, count)] = block.reshape(count, levels, gw)
        grad_ex[g].start()

    inv_copy.wait()
    steps = [(g, i) for g in range(groups) for i in range(qn)]
    for n, (g, i) in enumerate(steps):
        with jax.named_scope(f"unit{n}"):
            unit(g, i)
        pairs[n].start()
        if n > 0:
            combine(*steps[n - 1])
        with jax.named_scope(f"serve{n}"):
            if n == 3:
                serve_inner(0)
            if n == 5:
                serve_inner(1)
            if n == 6:
                serve_outer(0)
    with jax.named_scope("combine"):
        combine(*steps[-1])
    with jax.named_scope("serve_a"):
        serve_all(0)
        serve_all(1)
    with jax.named_scope("adjoint0"):
        adjoint(0)
    with jax.named_scope("serve_b"):
        serve_inner(2)
        serve_outer(1)
    with jax.named_scope("pass0"):
        gathers[0].pass_on()
    if groups > 1:
        with jax.named_scope("adjoint1"):
            adjoint(1)
    with jax.named_scope("serve_c"):
        serve_inner(3)
        serve_outer(2)
    with jax.named_scope("pass0l"):
        gathers[0].pass_last()
    with jax.named_scope("pass1"):
        gathers[1].pass_on()

    if line:
        def stage_of(c, j):
            return to(r.inc_out.at[c, j], r.inc_in.at[c, j], r.is_send.at[c, j], r.is_recv.at[c, j], mem=near)

        def cross_of(c, j):
            return to(r.inc_sum.at[c, j], r.inc_got.at[c, j], r.ic_send.at[c, j], r.ic_recv.at[c, j], mem=other)

        def final_of(c, j, where):
            return to(r.inc_all.at[c, j], r.inc_all.at[c, j], r.if_send.at[c, j], r.if_recv.at[c, j], mem=where)

    def spread(c, g):
        p = c * groups + g

        def part(j, carry):
            at = pl.ds(pl.multiple_of(j * width, width), width)
            cut = slice(g * gw, (g + 1) * gw)
            lhs = jnp.concatenate([r.pick[p, t] for t in range(sn)], axis=1)
            rhs = jnp.concatenate([r.base[t, cut, at] for t in range(sn)], axis=0)
            field = dot(lhs, rhs)
            if g > 0:
                field = field + r.acc[:, at]
            if g < groups - 1:
                r.acc[:, at] = field
                return carry
            run = jnp.zeros((lv, width), F32)
            for m in range(members):
                run = run + field[m * lv : (m + 1) * lv] * r.anom[m, c * lv : (c + 1) * lv, at].astype(F32)
            r.inc_part[c * lv : (c + 1) * lv, at] = run
            if line:

                @pl.when(outer)
                def _():
                    r.inc_out[c, j] = run.astype(BF16)
                    stage_of(c, j).start()

            return carry

        lax.fori_loop(0, STRIPS, part, 0)

    def each(fn):
        def step(j, carry):
            fn(j)
            return carry

        lax.fori_loop(0, STRIPS, step, 0)

    def inner_sum(c):
        def one(j):
            at = pl.ds(pl.multiple_of(j * width, width), width)
            stage_of(c, j).wait_recv()
            total = r.inc_part[c * lv : (c + 1) * lv, at] + r.inc_in[c, j].astype(F32)
            r.inc_sum[c, j] = total.astype(BF16)
            cross_of(c, j).start()

        if line:
            @pl.when(inner)
            def _():
                each(one)

    def inner_final(c):
        def one(j):
            cross_of(c, j).wait_recv()
            total = r.inc_sum[c, j].astype(F32) + r.inc_got[c, j].astype(F32)
            r.inc_all[c, j] = total.astype(BF16)
            final_of(c, j, rim).start()

        if line:
            @pl.when(inner)
            def _():
                each(one)

    def grad_inner(g):
        if line and g < groups:

            @pl.when(inner)
            def _():
                grad_ex[g].take_inner()

    with jax.named_scope("fin0"):
        gathers[0].finish()
    with jax.named_scope("spread0"):
        spread(0, 0)
    with jax.named_scope("serve_d"):
        serve_outer(3)
    if groups > 1:
        with jax.named_scope("pass1l"):
            gathers[1].pass_last()
            gathers[1].finish()
        with jax.named_scope("spread1"):
            spread(0, 1)
        with jax.named_scope("grad0"):
            grad_inner(0)
        with jax.named_scope("pass2"):
            gathers[2].pass_on()
            gathers[2].pass_last()
            gathers[2].finish()
        with jax.named_scope("spread2"):
            spread(1, 0)
        with jax.named_scope("sum0"):
            inner_sum(0)
        with jax.named_scope("pass3"):
            gathers[3].pass_on()
        with jax.named_scope("grad1"):
            grad_inner(1)
        with jax.named_scope("pass3l"):
            gathers[3].pass_last()
            gathers[3].finish()
        with jax.named_scope("spread3"):
            spread(1, 1)
    else:
        gathers[1].pass_last()
        gathers[1].finish()
        spread(1, 0)
        grad_inner(0)
        inner_sum(0)
    with jax.named_scope("final0"):
        inner_final(0)
    with jax.named_scope("sum1"):
        inner_sum(1)
    with jax.named_scope("final1"):
        inner_final(1)

    with jax.named_scope("settle"):
        if line:
            @pl.when(outer)
            def _():
                for ex in grad_ex:
                    ex.take_outer()
        else:
            for ex in grad_ex:
                ex.take()
        for g in range(groups):
            grad_out[:, g * gw : (g + 1) * gw] = r.got[g]

    if line:
        with jax.named_scope("last"):
            @pl.when(outer)
            def _():
                for c in range(HALVES):
                    each(lambda j, c=c: final_of(c, j, near).wait_recv())

            for c in range(HALVES):
                for j in range(STRIPS):
                    inc_out[c * lv : (c + 1) * lv, j * width : (j + 1) * width] = r.inc_all[c, j]

        @pl.when(outer)
        def _():
            for c in range(HALVES):
                each(lambda j, c=c: stage_of(c, j).wait_send())

        @pl.when(inner)
        def _():
            for c in range(HALVES):
                each(lambda j, c=c: cross_of(c, j).wait_send())
                each(lambda j, c=c: final_of(c, j, rim).wait_send())
    else:
        strip = columns // zn
        sums = [
            to(r.inc_out.at[k], r.inc_in.at[k], r.is_send.at[k], r.is_recv.at[k], mem=zpeer[k]) for k in range(1, zn)
        ]
        for k in range(1, zn):
            at = pl.ds(pl.multiple_of(zpeer[k] * strip, strip), strip)
            r.inc_out[k] = r.inc_part[:, at].astype(BF16)
            sums[k - 1].start()
        run = r.inc_part[:, pl.ds(pl.multiple_of(z * strip, strip), strip)]
        for k in range(1, zn):
            sums[k - 1].wait_recv()
            run = run + r.inc_in[k].astype(F32)
        r.inc_all[z] = run.astype(BF16)

        def held(k, a):
            return to(r.inc_all.at[a], r.inc_all.at[a], r.if_send.at[k], r.if_recv.at[a], mem=zpeer[k])

        shares = [held(k, z) for k in range(1, zn)]
        for copy in shares:
            copy.start()
        for k in range(1, zn):
            held(k, zpeer[k]).wait_recv()
        for b in range(zn):
            inc_out[:, b * strip : (b + 1) * strip] = r.inc_all[b]
        for copy in sums + shares:
            copy.wait_send()

    with jax.named_scope("drain"):
        for ex in coef_ex + grad_ex:
            ex.drain()
        for gather in gathers:
            gather.drain()
        for copy in pairs + [c for some in scatters for c in some]:
            copy.wait_send()


def widen(inc, grad, inc_out, grad_out):
    inc_out[...] = inc[...].astype(F32)
    grad_out[...] = grad[...].astype(F32)


def on_device(zn, sn, anomalies, alpha, basis, gradient, vertical_root, band_gain, band, order):
    members, levels, columns = anomalies.shape
    modes = alpha.shape[2]
    rows = members * levels
    qn = sn // 2
    slots = zn * members
    gw = min(LANES, modes)
    groups = modes // gw
    lv = levels // HALVES
    parts = HALVES * groups
    arrivals = 2 if qn == 4 else qn - 1
    width = columns // STRIPS
    line = zn == 4
    vmem = pl.BlockSpec(memory_space=pltpu.VMEM)
    smem = pl.BlockSpec(memory_space=pltpu.SMEM)
    hbm = pl.BlockSpec(memory_space=pl.ANY)
    dma = pltpu.SemaphoreType.DMA
    lookup = (1, -(-slots // LANES) * LANES)
    scratch = dict(
        anom=pltpu.VMEM((members, levels, columns), BF16),
        base=pltpu.VMEM((sn, modes, columns), BF16),
        weighted=pltpu.VMEM((rows, columns), BF16),
        alpha=pltpu.VMEM((rows, modes), BF16),
        gradient=pltpu.VMEM((levels, columns), BF16),
        vroot=pltpu.VMEM((levels, levels), F32),
        band=pltpu.VMEM((modes,), jnp.int32),
        gain=pltpu.VMEM((1, modes), F32),
        root_t=pltpu.VMEM((2, GROUP, GROUP), BF16),
        inv_v=pltpu.VMEM(lookup, jnp.int32),
        inv_s=pltpu.SMEM(lookup, jnp.int32),
        coef_pack=pltpu.VMEM((parts, members * lv, gw), BF16),
        pick=pltpu.VMEM((parts, sn, members * lv, gw), BF16),
        pair_out=pltpu.VMEM((groups * qn, rows, gw), F32),
        pair_in=pltpu.VMEM((groups * qn, rows, gw), F32),
        mine=pltpu.VMEM((groups * qn, rows, gw), F32),
        rs_out=pltpu.VMEM((groups, qn - 1, rows, gw), BF16),
        rs_in=pltpu.VMEM((groups, arrivals, rows, gw), BF16),
        relay_in=pltpu.VMEM((groups, rows, gw), BF16),
        grad_pack=pltpu.VMEM((groups, rows, gw), BF16),
        got=pltpu.VMEM((groups, rows, gw), BF16),
        acc=pltpu.VMEM((members * lv, columns), F32),
        inc_part=pltpu.VMEM((levels, columns), F32),
        load_sem=dma((5,)),
        base_sem=dma((groups * sn,)),
        inv_sem=dma,
        z_send=dma((parts, zn)),
        z_recv=dma((parts, zn)),
        g_send=dma((groups, zn)),
        g_recv=dma((groups, zn)),
        pk_send=dma((parts, sn)),
        pk_recv=dma((parts, sn)),
        pair_send=dma((groups * qn,)),
        pair_recv=dma((groups * qn,)),
        rs_send=dma((groups, qn - 1)),
        rs_recv=dma((groups, qn - 1)),
    )
    scratch |= {f"coef_held{p}": pltpu.VMEM((slots, lv, gw), BF16) for p in range(parts)}
    scratch |= {f"grad_held{g}": pltpu.VMEM((slots, levels, gw), BF16) for g in range(groups)}
    if line:
        strips = (HALVES, STRIPS, lv, width)
        scratch |= {n: pltpu.VMEM(strips, BF16) for n in ("inc_out", "inc_in", "inc_sum", "inc_got", "inc_all")}
        signals = ("is_send", "is_recv", "ic_send", "ic_recv", "if_send", "if_recv")
        scratch |= {n: dma((HALVES, STRIPS)) for n in signals}
    else:
        strips = (zn, levels, columns // zn)
        scratch |= {n: pltpu.VMEM(strips, BF16) for n in ("inc_out", "inc_in", "inc_all")}
        scratch |= {n: dma((zn,)) for n in ("is_send", "is_recv", "if_send", "if_recv")}
    increment, grads = pl.pallas_call(
        functools.partial(kernel, zn, sn, tuple(scratch)),
        out_shape=(
            jax.ShapeDtypeStruct((levels, columns), BF16),
            jax.ShapeDtypeStruct((rows, modes), BF16),
        ),
        in_specs=[smem] * 2 + [hbm] * 6,
        out_specs=(vmem, vmem),
        scratch_shapes=list(scratch.values()),
        compiler_params=pltpu.CompilerParams(
            collective_id=0, has_side_effects=True, vmem_limit_bytes=58 * 2**20
        ),
    )(
        order, band_gain, vertical_root, alpha.reshape(rows, modes), band, gradient,
        anomalies, basis.reshape(sn, modes, columns),
    )
    increment, grads = pl.pallas_call(
        widen,
        out_shape=(
            jax.ShapeDtypeStruct((levels, columns), F32),
            jax.ShapeDtypeStruct((rows, modes), F32),
        ),
        in_specs=[vmem] * 2,
        out_specs=(vmem, vmem),
    )(increment, grads)
    return increment, grads.reshape(members, levels, modes)


def solution(mesh):
    zn, sn = mesh.shape["mem"], mesh.shape["state"]
    return jax.shard_map(
        functools.partial(on_device, zn, sn),
        mesh=mesh,
        in_specs=(
            P("mem", None, "state"),
            P("mem", None, "state"),
            P(None, "state"),
            P(None, "state"),
            P(),
            P(),
            P("state"),
            P(),
        ),
        out_specs=(P(None, "state"), P("mem", None, "state")),
        check_vma=False,
    )
```

time: 69.9 us -> 73.7 us (1.054)
  Pallas kernels: 62.2 us -> 72.9 us
  other arithmetic: 6.91 us -> 0 us
    pallas_call x1 -> x2, Pallas kernels: 62.2 us -> 72.9 us  [the longest x1 70.9 us: on_device(): pl.pallas_call(functools.partial(kernel, zn, sn, tuple(scratch)), out_sha...]
    reduce_sum x2 -> x0, other arithmetic: 2.1 us -> none  [the longest x1 1.34 us: on_device(): gain = jnp.sum(onehot * band_gain[None, :], axis=1)[None, :]]
    reshape x1 -> x0, other arithmetic: 1.79 us -> none  [on_device(): grads.astype(F32).reshape(members, levels, mode_rows)]
    convert_element_type x1 -> x0, other arithmetic: 1.78 us -> none  [on_device(): increment.astype(F32)]
    another operation x1 -> x0, other arithmetic: 1.23 us -> none  [on_device(): table = jnp.stack([slot_of, order])]
where the time goes in v1:
time: 73.7 us; the launch traced here: 73.6 us
  Pallas kernels  72.9 us (99%)
    pallas_call x1, Pallas kernels, on_device(): pl.pallas_call(functools.partial(kernel, zn, sn, tuple(scratch)), out_sha...  70.9 us
    pallas_call x1, Pallas kernels, on_device(): pl.pallas_call(widen, out_shape=(jax.ShapeDtypeStruct((levels, columns),...  2.03 us

profile of v1, /device:TPU:0, one launch (start us, length us, event | category | flops | bytes accessed | tf_op | source)
XLA Modules:
  0.0 73.6 jit_solution(3279720378293355463)
XLA Ops:
  0.6 70.9 %shard_map.95 = (bf16[32,4096]{1,0:T(8,128)(2,1)}, bf16[512,256]{1,0:T(8,128)(2,1)}) custom-call(s32[64]{0:T(128)} %order.1, f32[16]{0:T(128)} %band_gain.1, f32[32,32]{1,0:T(8,128)} %vroot_h.1, bf16[512,256]{1,0:T(8,128)(2,1)} %bitcast.4, s32[256]{0:T(256)} %band_h.1, bf16[32,4096]{1,0:T(8,128)(2,1)} %gradient_h.1, bf16[16,32,4096]{2,1,0:T(8,128)(2,1)} %anomalies.1, ...), custom_call_target="tpu_custom_call" | custom-call | tf_op jit(solution)/shard_map/pallas_call | solution.py:699
  71.5 2.0 %shard_map.96 = (f32[32,4096]{1,0:T(8,128)}, f32[512,256]{1,0:T(8,128)}) custom-call(bf16[32,4096]{1,0:T(8,128)(2,1)} %get-tuple-element.6.inc, bf16[512,256]{1,0:T(8,128)(2,1)} %get-tuple-element.7.grad), custom_call_target="tpu_custom_call" | custom-call | tf_op jit(solution)/shard_map/pallas_call | solution.py:715

commit v2 on v1

--- a/solution.py
+++ b/solution.py
@@ -18,9 +18,9 @@
 
 
 def flip(a, k, n):
-    out, bit = 0, 1
+    out, bit, k = 0, 1, jnp.asarray(k, jnp.int32)
     while bit < n:
-        out = out + lax.rem(lax.div(a, bit) + (k // bit) % 2, 2) * bit
+        out = out + lax.rem(lax.div(a, bit) + lax.div(k, bit), 2) * bit
         bit *= 2
     return out
 
@@ -52,24 +52,24 @@
     slots = zn * members
     width = columns // STRIPS
     line, square = zn == 4, qn == 4
+    tuned = line and square and groups == 2
 
     zpeer = [flip(z, k, zn) for k in range(zn)]
     qpeer = [flip(chip, k, qn) for k in range(qn)]
     if square:
         first = qpeer[1] * (1 - core) + qpeer[2] * core
         second = qpeer[2] * (1 - core) + qpeer[1] * core
-        chips = [qpeer[3], first, second, chip]
-        chips_there = [qpeer[3], second, first, chip]
-    else:
-        chips = [qpeer[k] for k in range(qn - 1, -1, -1)]
-        chips_there = chips
-
-    barrier = pltpu.get_barrier_semaphore()
-    for k in range(1, zn):
-        pl.semaphore_signal(barrier, inc=1, device_id={"mem": zpeer[k]}, device_id_type=MESH)
-    for k in range(1, qn):
-        pl.semaphore_signal(barrier, inc=1, device_id={"state": qpeer[k] * 2 + core}, device_id_type=MESH)
-    pl.semaphore_signal(barrier, inc=1, device_id={"state": partner}, device_id_type=MESH)
+
+    def chip_at(i, side):
+        if square:
+            i = side * i + (1 - side) * (lax.rem(i, 2) * 2 + lax.div(i, 2))
+        return flip(chip, qn - 1 - i, qn)
+
+    def own_block(i):
+        return chip_at(i, core) * 2 + core
+
+    def other_block(i):
+        return chip_at(i, 1 - core) * 2 + 1 - core
 
     small = [
         pltpu.make_async_copy(src, dst, r.load_sem.at[i])
@@ -80,17 +80,25 @@
     for copy in small:
         copy.start()
 
+    barrier = pltpu.get_barrier_semaphore()
+    for k in range(1, zn):
+        pl.semaphore_signal(barrier, inc=1, device_id={"mem": zpeer[k]}, device_id_type=MESH)
+    for k in range(1, qn):
+        pl.semaphore_signal(barrier, inc=1, device_id={"state": qpeer[k] * 2 + core}, device_id_type=MESH)
+    pl.semaphore_signal(barrier, inc=1, device_id={"state": partner}, device_id_type=MESH)
+
+    def mode_rows(g):
+        return pl.ds(pl.multiple_of(g * gw, gw), gw)
+
     def load_of(g, t, n):
-        here = pl.ds(g * gw, gw)
+        here = mode_rows(g)
         return pltpu.make_async_copy(basis.at[t, here], r.base.at[t, here], r.base_sem.at[n])
 
-    loads = []
-    for g in range(groups):
-        for i in range(qn):
-            n = 2 * (g * qn + i)
-            loads.append((load_of(g, chips_there[i] * 2 + 1 - core, n), load_of(g, chips[i] * 2 + core, n + 1)))
-            loads[-1][0].start()
-            loads[-1][1].start()
+    def loads_of(n):
+        i, g = lax.div(n, groups), lax.rem(n, groups)
+        return load_of(g, other_block(i), 2 * n), load_of(g, own_block(i), 2 * n + 1)
+
+    units = groups * qn
 
     def to(src, dst, send, recv, **where):
         return pltpu.make_async_remote_copy(
@@ -215,6 +223,13 @@
             r.root_t[keep] = v
         small[1].wait()
         small[2].wait()
+
+        def load(n, carry):
+            for copy in loads_of(n):
+                copy.start()
+            return carry
+
+        lax.fori_loop(0, units, load, 0)
         band = r.band[...].reshape(1, modes)
         gain = jnp.zeros((1, modes), F32)
         for b in range(band_gain.shape[0]):
@@ -269,21 +284,10 @@
 
     class Gather:
         def __init__(self, p):
-            self.p = p
-            if square:
-                self.out = [
-                    share(p, s, 0, first * 2 + core), share(p, s, 1, second * 2 + core), share(p, s, 2, partner)
-                ]
-                tf, ts, td = first * 2 + core, second * 2 + core, qpeer[3] * 2 + core
-                self.relay = share(p, tf, 3, second * 2 + core)
-                self.arrive = [share(p, t, 4, partner) for t in (tf, ts, td)]
-                self.over = [share(p, t, 4 + i, partner) for i, t in enumerate((tf, ts, td))]
-            else:
-                self.out = [share(p, s, k - 1, qpeer[k] * 2 + core) for k in range(1, qn)]
-                self.out.append(share(p, s, qn - 1, partner))
-                blocks_there = [qpeer[k] * 2 + core for k in range(1, qn)]
-                self.arrive = [share(p, t, qn, partner) for t in blocks_there]
-                self.over = [share(p, t, qn + i, partner) for i, t in enumerate(blocks_there)]
+            there = [qpeer[k] * 2 + core for k in range(1, qn)]
+            self.out = [share(p, s, i, where) for i, where in enumerate(there)]
+            self.out.append(share(p, s, qn - 1, partner))
+            self.over = [share(p, t, qn + i, partner) for i, t in enumerate(there)]
             self.rest = [share(p, qpeer[k] * 2 + 1 - core, 0, partner) for k in range(qn)]
 
         def start(self):
@@ -291,99 +295,79 @@
                 copy.start()
 
         def pass_on(self):
-            if square:
-                self.arrive[0].wait_recv()
-                self.relay.start()
-                self.over[0].start()
-                self.arrive[1].wait_recv()
-                self.over[1].start()
-            else:
-                for come, go in zip(self.arrive, self.over):
-                    come.wait_recv()
-                    go.start()
-
-        def pass_last(self):
-            if square:
-                self.arrive[2].wait_recv()
-                self.over[2].start()
+            for copy in self.over:
+                copy.wait_recv()
+                copy.start()
 
         def finish(self):
             for copy in self.rest:
                 copy.wait_recv()
 
         def drain(self):
-            for copy in self.out + self.over + ([self.relay] if square else []):
+            for copy in self.out + self.over:
                 copy.wait_send()
 
     gathers = [Gather(p) for p in range(parts)]
 
-    def serve_inner(p):
-        if line and p < parts:
-
-            @pl.when(inner)
-            def _():
-                coef_ex[p].take_inner()
-                gathers[p].start()
-
-    def serve_outer(p):
-        if line and p < parts:
-
-            @pl.when(outer)
-            def _():
-                coef_ex[p].take_outer()
-                gathers[p].start()
-
-    def serve_all(p):
-        if not line and p < parts:
-            coef_ex[p].take()
-            gathers[p].start()
-
-    pairs = [
-        to(r.pair_out.at[n], r.pair_in.at[n], r.pair_send.at[n], r.pair_recv.at[n], state=partner)
-        for n in range(groups * qn)
-    ]
-    scatters = []
-    for g in range(groups):
-        if square:
-            via = [(r.relay_in.at[g], first), (r.rs_in.at[g, 0], first), (r.rs_in.at[g, 1], second)]
-        else:
-            via = [(r.rs_in.at[g, i], chips[i]) for i in range(qn - 1)]
-        scatters.append([
-            to(r.rs_out.at[g, i], dst, r.rs_send.at[g, i], r.rs_recv.at[g, i], state=where * 2 + core)
-            for i, (dst, where) in enumerate(via)
-        ])
-
-    def unit(g, i):
-        n = g * qn + i
-        for copy in loads[n]:
-            copy.wait()
-        cut = slice(g * gw, (g + 1) * gw)
-        rhs = jnp.concatenate(
-            [r.base[chips_there[i] * 2 + 1 - core, cut, :], r.base[chips[i] * 2 + core, cut, :]], axis=0
-        )
-        both = dot_nt(r.weighted[...], rhs)
-        r.pair_out[n] = both[:, :gw]
-        r.mine[n] = both[:, gw:]
-
-    def combine(g, i):
-        n = g * qn + i
-        pairs[n].wait_recv()
-        total = r.mine[n] + r.pair_in[n]
-        if i == qn - 1:
-            r.mine[n] = total
-            return
-        if square and i == 2:
-            scatters[g][0].wait_recv()
-            total = total + r.relay_in[g].astype(F32)
-        r.rs_out[g, i] = total.astype(BF16)
-        scatters[g][i].start()
+    def on_inner(*fns):
+        def run():
+            for fn in fns:
+                fn()
+
+        if line:
+            pl.when(inner)(run)
+
+    def on_outer(*fns):
+        def run():
+            for fn in fns:
+                fn()
+
+        if line:
+            pl.when(outer)(run)
+
+    def pair_of(n):
+        return to(r.pair_out.at[n], r.pair_in.at[n], r.pair_send.at[n], r.pair_recv.at[n], state=partner)
+
+    def scatter(g, i, dst, where):
+        n = i * groups + g
+        return to(r.rs_out.at[n], dst, r.rs_send.at[n], r.rs_recv.at[n], state=where * 2 + core)
+
+    def scatters_of(g):
+        if not square:
+            return [scatter(g, i, r.rs_in.at[g * (qn - 1) + i], chip_at(i, core)) for i in range(qn - 1)]
+        return [
+            scatter(g, 0, r.relay_in.at[g], first),
+            scatter(g, 1, r.rs_in.at[g * 2], first),
+            scatter(g, 2, r.rs_in.at[g * 2 + 1], second),
+        ]
+
+    def combine(n):
+        i, g = lax.div(n, groups), lax.rem(n, groups)
+        pair_of(n).wait_recv()
+
+        @pl.when(i == qn - 1)
+        def _():
+            r.mine[n] = r.mine[n] + r.pair_in[n]
+
+        copies = scatters_of(g)
+        for k, copy in enumerate(copies):
+
+            @pl.when(i == k)
+            def _():
+                total = r.mine[n] + r.pair_in[n]
+                if square and k == 2:
+                    copies[0].wait_recv()
+                    total = total + r.relay_in[g].astype(F32)
+                r.rs_out[n] = total.astype(BF16)
+                copy.start()
 
     def adjoint(g):
-        for copy in scatters[g][1:] if square else scatters[g]:
+        scatters = scatters_of(g)[1:] if square else scatters_of(g)
+        for copy in scatters:
             copy.wait_recv()
-        total = r.mine[g * qn + qn - 1]
-        for i in range(r.rs_in.shape[1]):
-            total = total + r.rs_in[g, i].astype(F32)
+        total = r.mine[(qn - 1) * groups + g]
+        for i in range(len(scatters)):
+            total = total + r.rs_in[g * len(scatters) + i].astype(F32)
         stack = jnp.concatenate([total[n * GROUP : (n + 1) * GROUP] for n in range(rows // GROUP)], axis=1)
         high, low = split(stack)
         grad = dot(r.root_t[0], high) + dot(r.root_t[0], low) + dot(r.root_t[1], high)
@@ -395,43 +379,36 @@
         grad_ex[g].start()
 
     inv_copy.wait()
-    steps = [(g, i) for g in range(groups) for i in range(qn)]
-    for n, (g, i) in enumerate(steps):
-        with jax.named_scope(f"unit{n}"):
-            unit(g, i)
-        pairs[n].start()
-        if n > 0:
-            combine(*steps[n - 1])
-        with jax.named_scope(f"serve{n}"):
-            if n == 3:
-                serve_inner(0)
-            if n == 5:
-                serve_inner(1)
-            if n == 6:
-                serve_outer(0)
-    with jax.named_scope("combine"):
-        combine(*steps[-1])
-    with jax.named_scope("serve_a"):
-        serve_all(0)
-        serve_all(1)
-    with jax.named_scope("adjoint0"):
-        adjoint(0)
-    with jax.named_scope("serve_b"):
-        serve_inner(2)
-        serve_outer(1)
-    with jax.named_scope("pass0"):
-        gathers[0].pass_on()
-    if groups > 1:
-        with jax.named_scope("adjoint1"):
-            adjoint(1)
-    with jax.named_scope("serve_c"):
-        serve_inner(3)
-        serve_outer(2)
-    with jax.named_scope("pass0l"):
-        gathers[0].pass_last()
-    with jax.named_scope("pass1"):
-        gathers[1].pass_on()
-
+    take_in = [ex.take_inner for ex in coef_ex] if line else []
+    take_out = [ex.take_outer for ex in coef_ex] if line else []
+    services = {
+        2: lambda: on_inner(take_in[0]),
+        4: lambda: on_inner(take_in[1]),
+        6: lambda: on_inner(take_in[2]),
+    }
+
+    def unit(n, carry):
+        i = lax.div(n, groups)
+        cut = mode_rows(lax.rem(n, groups))
+        for copy in loads_of(n):
+            copy.wait()
+        with jax.named_scope("unit"):
+            rhs = jnp.concatenate([r.base[other_block(i), cut, :], r.base[own_block(i), cut, :]], axis=0)
+            both = dot_nt(r.weighted[...], rhs)
+            r.pair_out[n] = both[:, :gw]
+            r.mine[n] = both[:, gw:]
+        pair_of(n).start()
+
+        @pl.when(n > 0)
+        def _():
+            combine(n - 1)
+
+        if tuned:
+            for at, serve in services.items():
+                pl.when(n == at)(serve)
+        return carry
+
+    lax.fori_loop(0, units, unit, 0)
     if line:
         def stage_of(c, j):
             return to(r.inc_out.at[c, j], r.inc_in.at[c, j], r.is_send.at[c, j], r.is_recv.at[c, j], mem=near)
@@ -442,7 +419,7 @@
         def final_of(c, j, where):
             return to(r.inc_all.at[c, j], r.inc_all.at[c, j], r.if_send.at[c, j], r.if_recv.at[c, j], mem=where)
 
-    def spread(c, g):
+    def spread(c, g, hooks={}):
         p = c * groups + g
 
         def part(j, carry):
@@ -453,6 +430,8 @@
             field = dot(lhs, rhs)
             if g > 0:
                 field = field + r.acc[:, at]
+            for k, hook in hooks.items():
+                pl.when(j == k)(hook)
             if g < groups - 1:
                 r.acc[:, at] = field
                 return carry
@@ -510,49 +489,56 @@
             def _():
                 grad_ex[g].take_inner()
 
-    with jax.named_scope("fin0"):
-        gathers[0].finish()
-    with jax.named_scope("spread0"):
-        spread(0, 0)
-    with jax.named_scope("serve_d"):
-        serve_outer(3)
-    if groups > 1:
-        with jax.named_scope("pass1l"):
-            gathers[1].pass_last()
-            gathers[1].finish()
-        with jax.named_scope("spread1"):
-            spread(0, 1)
-        with jax.named_scope("grad0"):
-            grad_inner(0)
-        with jax.named_scope("pass2"):
-            gathers[2].pass_on()
-            gathers[2].pass_last()
-            gathers[2].finish()
-        with jax.named_scope("spread2"):
-            spread(1, 0)
-        with jax.named_scope("sum0"):
-            inner_sum(0)
-        with jax.named_scope("pass3"):
-            gathers[3].pass_on()
-        with jax.named_scope("grad1"):
-            grad_inner(1)
-        with jax.named_scope("pass3l"):
-            gathers[3].pass_last()
-            gathers[3].finish()
-        with jax.named_scope("spread3"):
-            spread(1, 1)
+    def scoped(name, *fns):
+        with jax.named_scope(name):
+            for fn in fns:
+                fn()
+
+    if tuned:
+        scoped("start0", lambda: on_outer(take_out[0]), gathers[0].start)
+        scoped("inner3", lambda: on_inner(take_in[3], gathers[1].start))
+        scoped("combine", lambda: combine(jnp.int32(units - 1)))
+        scoped("adjoint0", lambda: adjoint(0))
+        scoped("start1", lambda: on_outer(take_out[1], gathers[1].start))
+        scoped("adjoint1", lambda: adjoint(1))
+        scoped("start2", lambda: on_outer(take_out[2]), gathers[2].start)
+        scoped("pass0", gathers[0].pass_on)
+        scoped("fin0", gathers[0].finish)
+        scoped("spread0", lambda: spread(0, 0, {
+            0: lambda: on_inner(gathers[3].start),
+            1: lambda: on_outer(take_out[3], gathers[3].start),
+            2: gathers[1].pass_on,
+        }))
+        scoped("fin1", gathers[1].finish)
+        scoped("spread1", lambda: spread(0, 1, {2: gathers[2].pass_on}))
+        scoped("grad0", lambda: grad_inner(0))
+        scoped("fin2", gathers[2].finish)
+        scoped("spread2", lambda: spread(1, 0, {2: gathers[3].pass_on, 3: lambda: inner_sum(0)}))
+        scoped("grad1", lambda: grad_inner(1))
+        scoped("fin3", gathers[3].finish)
+        scoped("spread3", lambda: spread(1, 1, {3: lambda: inner_final(0)}))
+        scoped("sum1", lambda: inner_sum(1))
+        scoped("final1", lambda: inner_final(1))
     else:
-        gathers[1].pass_last()
-        gathers[1].finish()
-        spread(1, 0)
-        grad_inner(0)
-        inner_sum(0)
-    with jax.named_scope("final0"):
-        inner_final(0)
-    with jax.named_scope("sum1"):
-        inner_sum(1)
-    with jax.named_scope("final1"):
-        inner_final(1)
+        combine(jnp.int32(units - 1))
+        for p in range(parts):
+            if line:
+                on_inner(take_in[p])
+                on_outer(take_out[p])
+            else:
+                coef_ex[p].take()
+            gathers[p].start()
+        for g in range(groups):
+            adjoint(g)
+        for c in range(HALVES):
+            for g in range(groups):
+                gathers[c * groups + g].pass_on()
+                gathers[c * groups + g].finish()
+                spread(c, g)
+            inner_sum(c)
+            inner_final(c)
+        for g in range(groups):
+            grad_inner(g)
 
     with jax.named_scope("settle"):
         if line:
@@ -620,8 +606,11 @@
             ex.drain()
         for gather in gathers:
             gather.drain()
-        for copy in pairs + [c for some in scatters for c in some]:
-            copy.wait_send()
+        for n in range(units):
+            pair_of(n).wait_send()
+        for g in range(groups):
+            for copy in scatters_of(g):
+                copy.wait_send()
 
 
 def widen(inc, grad, inc_out, grad_out):
@@ -664,8 +653,8 @@
         pair_out=pltpu.VMEM((groups * qn, rows, gw), F32),
         pair_in=pltpu.VMEM((groups * qn, rows, gw), F32),
         mine=pltpu.VMEM((groups * qn, rows, gw), F32),
-        rs_out=pltpu.VMEM((groups, qn - 1, rows, gw), BF16),
-        rs_in=pltpu.VMEM((groups, arrivals, rows, gw), BF16),
+        rs_out=pltpu.VMEM((groups * qn, rows, gw), BF16),
+        rs_in=pltpu.VMEM((groups * arrivals, rows, gw), BF16),
         relay_in=pltpu.VMEM((groups, rows, gw), BF16),
         grad_pack=pltpu.VMEM((groups, rows, gw), BF16),
         got=pltpu.VMEM((groups, rows, gw), BF16),
@@ -682,8 +671,8 @@
         pk_recv=dma((parts, sn)),
         pair_send=dma((groups * qn,)),
         pair_recv=dma((groups * qn,)),
-        rs_send=dma((groups, qn - 1)),
-        rs_recv=dma((groups, qn - 1)),
+        rs_send=dma((groups * qn,)),
+        rs_recv=dma((groups * qn,)),
     )
     scratch |= {f"coef_held{p}": pltpu.VMEM((slots, lv, gw), BF16) for p in range(parts)}
     scratch |= {f"grad_held{g}": pltpu.VMEM((slots, levels, gw), BF16) for g in range(groups)}

time: 73.7 us -> 54.5 us (0.74)
  Pallas kernels: 72.9 us -> 53.6 us
    pallas_call x1, Pallas kernels: 70.9 us -> 51.6 us  [on_device(): pl.pallas_call(functools.partial(kernel, zn, sn, tuple(scratch)), out_sha...]
where the time goes in v2:
time: 54.5 us; the launch traced here: 54.2 us
  Pallas kernels  53.6 us (98%)
  between operations  0.64 us (1%)
    pallas_call x1, Pallas kernels, on_device(): pl.pallas_call(functools.partial(kernel, zn, sn, tuple(scratch)), out_sha...  51.6 us
    pallas_call x1, Pallas kernels, on_device(): pl.pallas_call(widen, out_shape=(jax.ShapeDtypeStruct((levels, columns),...  2.03 us

profile of v2, /device:TPU:0, one launch (start us, length us, event | category | flops | bytes accessed | tf_op | source)
XLA Modules:
  0.0 54.2 jit_solution(9843442460504044801)
XLA Ops:
  0.6 51.6 %shard_map.95 = (bf16[32,4096]{1,0:T(8,128)(2,1)}, bf16[512,256]{1,0:T(8,128)(2,1)}) custom-call(s32[64]{0:T(128)} %order.1, f32[16]{0:T(128)} %band_gain.1, f32[32,32]{1,0:T(8,128)} %vroot_h.1, bf16[512,256]{1,0:T(8,128)(2,1)} %bitcast.4, s32[256]{0:T(256)} %band_h.1, bf16[32,4096]{1,0:T(8,128)(2,1)} %gradient_h.1, bf16[16,32,4096]{2,1,0:T(8,128)(2,1)} %anomalies.1, ...), custom_call_target="tpu_custom_call" | custom-call | tf_op jit(solution)/shard_map/pallas_call | solution.py:688
  52.2 2.0 %shard_map.96 = (f32[32,4096]{1,0:T(8,128)}, f32[512,256]{1,0:T(8,128)}) custom-call(bf16[32,4096]{1,0:T(8,128)(2,1)} %get-tuple-element.6.inc, bf16[512,256]{1,0:T(8,128)(2,1)} %get-tuple-element.7.grad), custom_call_target="tpu_custom_call" | custom-call | tf_op jit(solution)/shard_map/pallas_call | solution.py:704

commit v3 on v2

--- a/solution.py
+++ b/solution.py
@@ -32,7 +32,7 @@
 
 def kernel(
     zn, sn, names,
-    order, band_gain, vroot_h, alpha_h, band_h, gradient_h, anomalies, basis,
+    order_h, band_gain_h, vroot_h, alpha_h, band_h, gradient_h, anomalies, basis,
     inc_out, grad_out, *scratch,
 ):
     r = types.SimpleNamespace(**dict(zip(names, scratch)))
@@ -74,7 +74,10 @@
     small = [
         pltpu.make_async_copy(src, dst, r.load_sem.at[i])
         for i, (src, dst) in enumerate(
-            [(vroot_h, r.vroot), (alpha_h, r.alpha), (band_h, r.band), (gradient_h, r.gradient), (anomalies, r.anom)]
+            [
+                (vroot_h, r.vroot), (alpha_h, r.alpha), (band_h, r.band), (band_gain_h, r.band_gain),
+                (order_h, r.order), (gradient_h, r.gradient), (anomalies, r.anom),
+            ]
         )
     ]
     for copy in small:
@@ -94,9 +97,13 @@
         here = mode_rows(g)
         return pltpu.make_async_copy(basis.at[t, here], r.base.at[t, here], r.base_sem.at[n])
 
+    def loaded(n):
+        two = (pl.ds(0, 2), pl.ds(0, gw))
+        return pltpu.make_async_copy(basis.at[two], r.base.at[two], r.base_sem.at[n])
+
     def loads_of(n):
         i, g = lax.div(n, groups), lax.rem(n, groups)
-        return load_of(g, other_block(i), 2 * n), load_of(g, own_block(i), 2 * n + 1)
+        return load_of(g, other_block(i), n), load_of(g, own_block(i), n)
 
     units = groups * qn
 
@@ -104,14 +111,6 @@
         return pltpu.make_async_remote_copy(
             src_ref=src, dst_ref=dst, send_sem=send, recv_sem=recv, device_id=where, device_id_type=MESH
         )
-
-    spot = lax.broadcasted_iota(jnp.int32, r.inv_v.shape, 1)
-    inverse = jnp.zeros(r.inv_v.shape, jnp.int32)
-    for j in range(slots):
-        inverse = jnp.where(spot == order[j], j, inverse)
-    r.inv_v[...] = inverse
-    inv_copy = pltpu.make_async_copy(r.inv_v, r.inv_s, r.inv_sem)
-    inv_copy.start()
 
     own_rows = pl.ds(z * members, members)
     outer = lax.div(lax.rem(z + 1, zn), 2) == 0
@@ -123,23 +122,28 @@
     distant = 3 - rim
 
     class Exchange:
-        def __init__(self, find, held, pack, mine, height, send, recv):
+        def __init__(self, find, held, pack, mine, height, send, recv, rim_recv=None):
             self.find, self.held, self.pack, self.mine, self.height = find, held, pack, mine, height
             own = held.at[own_rows]
+            come = held.at[pl.ds(0, (zn - 1) * members)]
+            self.come = to(come, come, send, recv, mem=zpeer[1])
+            gone = held.at[pl.ds(0, (2 if line else zn - 1) * members)]
+            self.gone = to(gone, gone, send, recv, mem=zpeer[1])
+            self.relayed, self.send = rim_recv is not None, send
             if not line:
-                self.out = [to(own, own, send.at[k], recv.at[z], mem=zpeer[k]) for k in range(1, zn)]
-                self.come = [self.arrival(zpeer[k], send, recv, zpeer[k]) for k in range(1, zn)]
+                self.out = [to(own, own, send, recv, mem=zpeer[k]) for k in range(1, zn)]
                 return
-            self.to_mid = to(own, own, send.at[0], recv.at[z], mem=mid)
-            self.to_near = to(own, own, send.at[1], recv.at[z], mem=near)
-            self.to_other = to(own, own, send.at[0], recv.at[z], mem=other)
-            self.give = to(pack, mine, send.at[2], recv.at[z], mem=rim)
-            self.given = to(pack, mine, send.at[2], recv.at[near], mem=near)
-            self.come = [self.arrival(a, send, recv, other) for a in (rim, other, distant)]
-
-        def arrival(self, a, send, recv, where):
-            there = self.held.at[pl.ds(a * members, members)]
-            return to(there, there, send.at[0], recv.at[a], mem=where)
+            self.to_mid = to(own, own, send, recv, mem=mid)
+            self.to_near = to(own, own, send, rim_recv if self.relayed else recv, mem=near)
+            self.to_other = to(own, own, send, recv, mem=other)
+            if self.relayed:
+                rims = held.at[pl.ds(rim * members, members)]
+                self.from_rim = to(rims, rims, send, rim_recv, mem=other)
+                self.hand_on = to(rims, rims, send, recv, mem=other)
+                count = pl.ds(0, 2 * members)
+                self.come = to(held.at[count], held.at[count], send, recv, mem=other)
+            self.give = to(pack, mine, send, recv, mem=rim)
+            self.given = to(pack, mine, send, recv, mem=near)
 
         def start(self):
             if not line:
@@ -149,7 +153,8 @@
 
             @pl.when(outer)
             def _():
-                self.to_mid.start()
+                if not self.relayed:
+                    self.to_mid.start()
                 self.to_near.start()
 
             @pl.when(inner)
@@ -161,8 +166,7 @@
                 out[m * self.height : (m + 1) * self.height, :] = self.held[self.find(who * members + m)]
 
         def take_inner(self):
-            for copy in self.come:
-                copy.wait_recv()
+            self.come.wait_recv()
             self.choose(self.pack, rim)
             self.give.start()
             self.choose(self.mine, z)
@@ -171,25 +175,26 @@
             self.given.wait_recv()
 
         def take(self):
-            for copy in self.come:
-                copy.wait_recv()
+            self.come.wait_recv()
             self.choose(self.mine, z)
 
+        def relay(self):
+            self.from_rim.wait_recv()
+            self.hand_on.start()
+
         def drain(self):
-            if not line:
-                for copy in self.out:
-                    copy.wait_send()
+            if not (line and self.relayed):
+                self.gone.wait_send()
                 return
 
             @pl.when(outer)
             def _():
-                self.to_mid.wait_send()
                 self.to_near.wait_send()
 
             @pl.when(inner)
             def _():
-                self.to_other.wait_send()
-                self.give.wait_send()
+                three = self.held.at[pl.ds(0, 3 * members)]
+                to(three, three, self.send, self.send, mem=other).wait_send()
 
     grid = (GROUP, levels)
     row_of = lax.broadcasted_iota(jnp.int32, grid, 0)
@@ -218,11 +223,9 @@
         small[0].wait()
         root_terms = split(r.vroot[...])
         root = [blocks(dot(pieced, v), same_pieced) for v in root_terms]
-        root_t = [blocks(dot_nt(plain, v), same_plain) for v in root_terms]
-        for v, keep in zip(root_t, (0, 1)):
-            r.root_t[keep] = v
         small[1].wait()
         small[2].wait()
+        small[3].wait()
 
         def load(n, carry):
             for copy in loads_of(n):
@@ -232,8 +235,8 @@
         lax.fori_loop(0, units, load, 0)
         band = r.band[...].reshape(1, modes)
         gain = jnp.zeros((1, modes), F32)
-        for b in range(band_gain.shape[0]):
-            gain = jnp.where(band == b, band_gain[b], gain)
+        for b in range(r.band_gain.shape[0]):
+            gain = jnp.where(band == b, r.band_gain[b], gain)
         r.gain[...] = gain
         for n in range(rows // GROUP):
             control = r.alpha[n * GROUP : (n + 1) * GROUP, :]
@@ -259,15 +262,27 @@
         ex.start()
     grad_ex = [
         Exchange(
-            lambda m: order[m], grad_held[g], r.grad_pack.at[g], r.got.at[g], levels,
-            r.g_send.at[g], r.g_recv.at[g],
+            lambda m: r.order[m], grad_held[g], r.grad_pack.at[g], r.got.at[g], levels,
+            r.g_send.at[g], r.g_recv.at[g], r.g_rim.at[g] if line else None,
         )
         for g in range(groups)
     ]
 
+    small[4].wait()
+    spot = lax.broadcasted_iota(jnp.int32, r.inv_v.shape, 1)
+    inverse = jnp.zeros(r.inv_v.shape, jnp.int32)
+    for j in range(slots):
+        inverse = jnp.where(spot == r.order[j], j, inverse)
+    r.inv_v[...] = inverse
+    inv_copy = pltpu.make_async_copy(r.inv_v, r.inv_s, r.inv_sem)
+    inv_copy.start()
+
+    for keep, v in enumerate(root_terms):
+        r.root_t[keep] = blocks(dot_nt(plain, v), same_plain)
+
     with jax.named_scope("weigh"):
-        small[3].wait()
-        small[4].wait()
+        small[5].wait()
+        small[6].wait()
 
         def weigh(m, carry):
             at = pl.ds(pl.multiple_of(m * levels, levels), levels)
@@ -279,33 +294,58 @@
     def block_of(p, t):
         return r.pick.at[p, t]
 
-    def share(p, t, i, where):
-        return to(block_of(p, t), block_of(p, t), r.pk_send.at[p, i], r.pk_recv.at[p, t], state=where)
+    def share(p, t, recv, where):
+        return to(block_of(p, t), block_of(p, t), r.pk_send.at[p], recv.at[p], state=where)
+
+    def several(p, count, recv):
+        some = r.pick.at[p, pl.ds(0, count)]
+        return to(some, some, r.pk_send.at[p], recv.at[p], state=partner)
 
     class Gather:
         def __init__(self, p):
             there = [qpeer[k] * 2 + core for k in range(1, qn)]
-            self.out = [share(p, s, i, where) for i, where in enumerate(there)]
-            self.out.append(share(p, s, qn - 1, partner))
-            self.over = [share(p, t, qn + i, partner) for i, t in enumerate(there)]
-            self.rest = [share(p, qpeer[k] * 2 + 1 - core, 0, partner) for k in range(qn)]
+            self.mate = share(p, partner, r.pk_mate, partner)
+            self.gone = several(p, 2 * qn - 1, r.pk_over)
+            if square:
+                side = [first * 2 + core, second * 2 + core]
+                self.out = [share(p, s, r.pk_side, where) for where in side]
+                self.relay = share(p, side[0], r.pk_far, side[1])
+                self.far = share(p, there[2], r.pk_far, partner)
+                self.far_over = share(p, there[2], r.pk_last, partner)
+                self.far_rest = share(p, there[2] + 1 - 2 * core, r.pk_last, partner)
+            else:
+                side = there
+                self.out = [share(p, s, r.pk_side, where) for where in side]
+            self.out.append(share(p, s, r.pk_mate, partner))
+            self.side = several(p, len(side), r.pk_side)
+            self.over = [share(p, t, r.pk_over, partner) for t in side]
+            self.rest = several(p, len(side), r.pk_over)
 
         def start(self):
             for copy in self.out:
                 copy.start()
 
         def pass_on(self):
+            self.side.wait_recv()
+            if square:
+                self.relay.start()
             for copy in self.over:
-                copy.wait_recv()
                 copy.start()
 
+        def pass_far(self):
+            if square:
+                self.far.wait_recv()
+                self.far_over.start()
+
         def finish(self):
-            for copy in self.rest:
-                copy.wait_recv()
+            self.rest.wait_recv()
+
+        def finish_far(self):
+            if square:
+                self.far_rest.wait_recv()
 
         def drain(self):
-            for copy in self.out + self.over:
-                copy.wait_send()
+            self.gone.wait_send()
 
     gathers = [Gather(p) for p in range(parts)]
 
@@ -326,20 +366,26 @@
             pl.when(outer)(run)
 
     def pair_of(n):
-        return to(r.pair_out.at[n], r.pair_in.at[n], r.pair_send.at[n], r.pair_recv.at[n], state=partner)
-
-    def scatter(g, i, dst, where):
-        n = i * groups + g
-        return to(r.rs_out.at[n], dst, r.rs_send.at[n], r.rs_recv.at[n], state=where * 2 + core)
+        return to(r.pair_out.at[n], r.pair_in.at[n], r.pair_send, r.pair_recv.at[n], state=partner)
+
+    def scatter(g, i, dst, recv, where):
+        return to(r.rs_out.at[i * groups + g], dst, r.rs_send, recv, state=where * 2 + core)
 
     def scatters_of(g):
+        recv = r.rs_recv.at[g]
         if not square:
-            return [scatter(g, i, r.rs_in.at[g * (qn - 1) + i], chip_at(i, core)) for i in range(qn - 1)]
+            return [scatter(g, i, r.rs_in.at[g * (qn - 1) + i], recv, chip_at(i, core)) for i in range(qn - 1)]
         return [
-            scatter(g, 0, r.relay_in.at[g], first),
-            scatter(g, 1, r.rs_in.at[g * 2], first),
-            scatter(g, 2, r.rs_in.at[g * 2 + 1], second),
+            scatter(g, 0, r.relay_in.at[g], r.relay_recv.at[g], first),
+            scatter(g, 1, r.rs_in.at[g * 2], recv, first),
+            scatter(g, 2, r.rs_in.at[g * 2 + 1], recv, second),
         ]
+
+    arrivals = r.rs_in.shape[0] // groups
+
+    def scattered(g):
+        block = r.rs_in.at[pl.ds(g * arrivals, arrivals)]
+        return to(block, block, r.rs_send, r.rs_recv.at[g], state=partner)
 
     def combine(n):
         i, g = lax.div(n, groups), lax.rem(n, groups)
@@ -362,12 +408,10 @@
                 copy.start()
 
     def adjoint(g):
-        scatters = scatters_of(g)[1:] if square else scatters_of(g)
-        for copy in scatters:
-            copy.wait_recv()
+        scattered(g).wait_recv()
         total = r.mine[(qn - 1) * groups + g]
-        for i in range(len(scatters)):
-            total = total + r.rs_in[g * len(scatters) + i].astype(F32)
+        for i in range(arrivals):
+            total = total + r.rs_in[g * arrivals + i].astype(F32)
         stack = jnp.concatenate([total[n * GROUP : (n + 1) * GROUP] for n in range(rows // GROUP)], axis=1)
         high, low = split(stack)
         grad = dot(r.root_t[0], high) + dot(r.root_t[0], low) + dot(r.root_t[1], high)
@@ -382,16 +426,16 @@
     take_in = [ex.take_inner for ex in coef_ex] if line else []
     take_out = [ex.take_outer for ex in coef_ex] if line else []
     services = {
-        2: lambda: on_inner(take_in[0]),
-        4: lambda: on_inner(take_in[1]),
-        6: lambda: on_inner(take_in[2]),
+        3: lambda: on_inner(take_in[0], gathers[0].start),
+        5: lambda: on_inner(take_in[1]),
+        6: lambda: on_outer(take_out[0], gathers[0].start),
+        7: lambda: on_inner(take_in[2]),
     }
 
     def unit(n, carry):
         i = lax.div(n, groups)
         cut = mode_rows(lax.rem(n, groups))
-        for copy in loads_of(n):
-            copy.wait()
+        loaded(n).wait()
         with jax.named_scope("unit"):
             rhs = jnp.concatenate([r.base[other_block(i), cut, :], r.base[own_block(i), cut, :]], axis=0)
             both = dot_nt(r.weighted[...], rhs)
@@ -411,29 +455,36 @@
     lax.fori_loop(0, units, unit, 0)
     if line:
         def stage_of(c, j):
-            return to(r.inc_out.at[c, j], r.inc_in.at[c, j], r.is_send.at[c, j], r.is_recv.at[c, j], mem=near)
+            return to(r.inc_out.at[c, j], r.inc_in.at[c, j], r.inc_send.at[0], r.inc_recv.at[c, j], mem=near)
 
         def cross_of(c, j):
-            return to(r.inc_sum.at[c, j], r.inc_got.at[c, j], r.ic_send.at[c, j], r.ic_recv.at[c, j], mem=other)
+            return to(r.inc_sum.at[c, j], r.inc_got.at[c, j], r.inc_send.at[0], r.cross_recv.at[c, j], mem=other)
 
         def final_of(c, j, where):
-            return to(r.inc_all.at[c, j], r.inc_all.at[c, j], r.if_send.at[c, j], r.if_recv.at[c, j], mem=where)
-
-    def spread(c, g, hooks={}):
-        p = c * groups + g
-
+            return to(r.inc_all.at[c, j], r.inc_all.at[c, j], r.inc_send.at[1], r.inc_recv.at[c, j], mem=where)
+
+    def product(c, modes_of, at):
+        lhs = [r.pick[c * groups + g, t] for g, t in modes_of]
+        rhs = [r.base[t, g * gw : (g + 1) * gw, at] for g, t in modes_of]
+        return dot(jnp.concatenate(lhs, axis=1), jnp.concatenate(rhs, axis=0))
+
+    def pair_at(chips):
+        return [c * 2 + side for c in chips for side in range(2)]
+
+    home = pair_at([chip])
+    sides = pair_at([first, second]) if square else pair_at([qpeer[k] for k in range(1, qn)])
+    corner = pair_at([qpeer[3]]) if square else []
+
+    def spread(c, blocks, start, last, hooks={}):
         def part(j, carry):
-            at = pl.ds(pl.multiple_of(j * width, width), width)
-            cut = slice(g * gw, (g + 1) * gw)
-            lhs = jnp.concatenate([r.pick[p, t] for t in range(sn)], axis=1)
-            rhs = jnp.concatenate([r.base[t, cut, at] for t in range(sn)], axis=0)
-            field = dot(lhs, rhs)
-            if g > 0:
-                field = field + r.acc[:, at]
             for k, hook in hooks.items():
                 pl.when(j == k)(hook)
-            if g < groups - 1:
-                r.acc[:, at] = field
+            at = pl.ds(pl.multiple_of(j * width, width), width)
+            field = product(c, blocks, at)
+            if not start:
+                field = field + r.acc[c, :, at]
+            if not last:
+                r.acc[c, :, at] = field
                 return carry
             run = jnp.zeros((lv, width), F32)
             for m in range(members):
@@ -495,29 +546,58 @@
                 fn()
 
     if tuned:
-        scoped("start0", lambda: on_outer(take_out[0]), gathers[0].start)
-        scoped("inner3", lambda: on_inner(take_in[3], gathers[1].start))
+        def go(*fns):
+            def run():
+                for fn in fns:
+                    fn()
+
+            return run
+
+        def of(gs, blocks):
+            return [(g, t) for g in gs for t in blocks]
+
+        scoped("start1", lambda: on_outer(take_out[1]), gathers[1].start)
         scoped("combine", lambda: combine(jnp.int32(units - 1)))
+        scoped("mate", gathers[0].mate.wait_recv, gathers[1].mate.wait_recv)
+        scoped("home0", lambda: spread(0, of((0, 1), home), True, False, {
+            1: lambda: on_inner(take_in[3]),
+            2: go(lambda: on_outer(take_out[2]), gathers[2].start),
+            3: lambda: on_inner(gathers[3].start),
+        }))
         scoped("adjoint0", lambda: adjoint(0))
-        scoped("start1", lambda: on_outer(take_out[1], gathers[1].start))
         scoped("adjoint1", lambda: adjoint(1))
-        scoped("start2", lambda: on_outer(take_out[2]), gathers[2].start)
         scoped("pass0", gathers[0].pass_on)
+        scoped("home1", gathers[2].mate.wait_recv, lambda: spread(1, of((0,), home), True, False))
         scoped("fin0", gathers[0].finish)
-        scoped("spread0", lambda: spread(0, 0, {
-            0: lambda: on_inner(gathers[3].start),
-            1: lambda: on_outer(take_out[3], gathers[3].start),
-            2: gathers[1].pass_on,
+        scoped("side0", lambda: spread(0, of((0,), sides), False, False, {
+            0: lambda: on_outer(take_out[3], gathers[3].start),
+            1: gathers[1].pass_on,
         }))
+        scoped("far0", gathers[0].pass_far)
         scoped("fin1", gathers[1].finish)
-        scoped("spread1", lambda: spread(0, 1, {2: gathers[2].pass_on}))
-        scoped("grad0", lambda: grad_inner(0))
-        scoped("fin2", gathers[2].finish)
-        scoped("spread2", lambda: spread(1, 0, {2: gathers[3].pass_on, 3: lambda: inner_sum(0)}))
+        scoped("side1", lambda: spread(0, of((1,), sides), False, False, {
+            1: gathers[2].pass_on,
+            2: lambda: on_inner(grad_ex[0].relay),
+        }))
+        scoped("home2", gathers[3].mate.wait_recv, lambda: spread(1, of((1,), home), False, False, {
+            0: gathers[1].pass_far,
+        }))
+        scoped("finf0", gathers[0].finish_far, gathers[1].finish_far)
+        scoped("corner0", lambda: spread(0, of((0, 1), corner), False, True, {
+            1: gathers[3].pass_on,
+            2: lambda: on_inner(grad_ex[1].relay),
+            3: gathers[2].pass_far,
+        }))
+        scoped("fin23", gathers[2].finish, gathers[3].finish)
+        scoped("side23", lambda: spread(1, of((0, 1), sides), False, False, {
+            2: lambda: grad_inner(0),
+            3: gathers[3].pass_far,
+        }))
+        scoped("finf1", gathers[2].finish_far, gathers[3].finish_far)
+        scoped("corner1", lambda: spread(1, of((0, 1), corner), False, True, {1: lambda: inner_sum(0)}))
         scoped("grad1", lambda: grad_inner(1))
-        scoped("fin3", gathers[3].finish)
-        scoped("spread3", lambda: spread(1, 1, {3: lambda: inner_final(0)}))
         scoped("sum1", lambda: inner_sum(1))
+        scoped("final0", lambda: inner_final(0))
         scoped("final1", lambda: inner_final(1))
     else:
         combine(jnp.int32(units - 1))
@@ -530,14 +610,19 @@
             gathers[p].start()
         for g in range(groups):
             adjoint(g)
+        for gather in gathers:
+            gather.mate.wait_recv()
+            gather.pass_on()
+            gather.pass_far()
         for c in range(HALVES):
             for g in range(groups):
-                gathers[c * groups + g].pass_on()
                 gathers[c * groups + g].finish()
-                spread(c, g)
+                gathers[c * groups + g].finish_far()
+                spread(c, [(g, t) for t in home + sides + corner], g == 0, g == groups - 1)
             inner_sum(c)
             inner_final(c)
         for g in range(groups):
+            on_inner(grad_ex[g].relay)
             grad_inner(g)
 
     with jax.named_scope("settle"):
@@ -563,16 +648,11 @@
                 for j in range(STRIPS):
                     inc_out[c * lv : (c + 1) * lv, j * width : (j + 1) * width] = r.inc_all[c, j]
 
-        @pl.when(outer)
-        def _():
-            for c in range(HALVES):
-                each(lambda j, c=c: stage_of(c, j).wait_send())
+        to(r.inc_sum, r.inc_got, r.inc_send.at[0], r.inc_recv.at[0, 0], mem=zpeer[1]).wait_send()
 
         @pl.when(inner)
         def _():
-            for c in range(HALVES):
-                each(lambda j, c=c: cross_of(c, j).wait_send())
-                each(lambda j, c=c: final_of(c, j, rim).wait_send())
+            to(r.inc_all, r.inc_all, r.inc_send.at[1], r.inc_recv.at[0, 0], mem=rim).wait_send()
     else:
         strip = columns // zn
         sums = [
@@ -606,11 +686,9 @@
             ex.drain()
         for gather in gathers:
             gather.drain()
-        for n in range(units):
-            pair_of(n).wait_send()
-        for g in range(groups):
-            for copy in scatters_of(g):
-                copy.wait_send()
+        to(r.pair_out, r.pair_in, r.pair_send, r.pair_recv.at[0], state=partner).wait_send()
+        gone = r.rs_out.at[pl.ds(0, (qn - 1) * groups)]
+        to(gone, gone, r.rs_send, r.rs_recv.at[0], state=partner).wait_send()
 
 
 def widen(inc, grad, inc_out, grad_out):
@@ -632,7 +710,6 @@
     width = columns // STRIPS
     line = zn == 4
     vmem = pl.BlockSpec(memory_space=pltpu.VMEM)
-    smem = pl.BlockSpec(memory_space=pltpu.SMEM)
     hbm = pl.BlockSpec(memory_space=pl.ANY)
     dma = pltpu.SemaphoreType.DMA
     lookup = (1, -(-slots // LANES) * LANES)
@@ -658,29 +735,36 @@
         relay_in=pltpu.VMEM((groups, rows, gw), BF16),
         grad_pack=pltpu.VMEM((groups, rows, gw), BF16),
         got=pltpu.VMEM((groups, rows, gw), BF16),
-        acc=pltpu.VMEM((members * lv, columns), F32),
+        acc=pltpu.VMEM((HALVES, members * lv, columns), F32),
         inc_part=pltpu.VMEM((levels, columns), F32),
-        load_sem=dma((5,)),
-        base_sem=dma((groups * sn,)),
+        load_sem=dma((7,)),
+        band_gain=pltpu.SMEM(band_gain.shape, F32),
+        order=pltpu.SMEM(order.shape, jnp.int32),
+        base_sem=dma((groups * qn,)),
         inv_sem=dma,
-        z_send=dma((parts, zn)),
-        z_recv=dma((parts, zn)),
-        g_send=dma((groups, zn)),
-        g_recv=dma((groups, zn)),
-        pk_send=dma((parts, sn)),
-        pk_recv=dma((parts, sn)),
-        pair_send=dma((groups * qn,)),
+        z_send=dma((parts,)),
+        z_recv=dma((parts,)),
+        g_send=dma((groups,)),
+        g_recv=dma((groups,)),
+        g_rim=dma((groups,)),
+        pk_send=dma((parts,)),
+        pk_side=dma((parts,)),
+        pk_mate=dma((parts,)),
+        pk_over=dma((parts,)),
+        pk_far=dma((parts,)),
+        pk_last=dma((parts,)),
+        pair_send=dma,
         pair_recv=dma((groups * qn,)),
-        rs_send=dma((groups * qn,)),
-        rs_recv=dma((groups * qn,)),
+        rs_send=dma,
+        rs_recv=dma((groups,)),
+        relay_recv=dma((groups,)),
     )
     scratch |= {f"coef_held{p}": pltpu.VMEM((slots, lv, gw), BF16) for p in range(parts)}
     scratch |= {f"grad_held{g}": pltpu.VMEM((slots, levels, gw), BF16) for g in range(groups)}
     if line:
         strips = (HALVES, STRIPS, lv, width)
         scratch |= {n: pltpu.VMEM(strips, BF16) for n in ("inc_out", "inc_in", "inc_sum", "inc_got", "inc_all")}
-        signals = ("is_send", "is_recv", "ic_send", "ic_recv", "if_send", "if_recv")
-        scratch |= {n: dma((HALVES, STRIPS)) for n in signals}
+        scratch |= {"inc_send": dma((2,))} | {n: dma((HALVES, STRIPS)) for n in ("inc_recv", "cross_recv")}
     else:
         strips = (zn, levels, columns // zn)
         scratch |= {n: pltpu.VMEM(strips, BF16) for n in ("inc_out", "inc_in", "inc_all")}
@@ -691,7 +775,7 @@
             jax.ShapeDtypeStruct((levels, columns), BF16),
             jax.ShapeDtypeStruct((rows, modes), BF16),
         ),
-        in_specs=[smem] * 2 + [hbm] * 6,
+        in_specs=[hbm] * 8,
         out_specs=(vmem, vmem),
         scratch_shapes=list(scratch.values()),
         compiler_params=pltpu.CompilerParams(

time: 54.5 us -> 52.1 us (0.956)
  Pallas kernels: 53.6 us -> 51.2 us
    pallas_call x1, Pallas kernels: 51.6 us -> 49.2 us  [on_device(): pl.pallas_call(functools.partial(kernel, zn, sn, tuple(scratch)), out_sha...]
where the time goes in v3:
time: 52.1 us; the launch traced here: 51.9 us
  Pallas kernels  51.2 us (98%)
  between operations  0.64 us (1%)
    pallas_call x1, Pallas kernels, on_device(): pl.pallas_call(functools.partial(kernel, zn, sn, tuple(scratch)), out_sha...  49.2 us
    pallas_call x1, Pallas kernels, on_device(): pl.pallas_call(widen, out_shape=(jax.ShapeDtypeStruct((levels, columns),...  2.03 us

profile of v3, /device:TPU:0, one launch (start us, length us, event | category | flops | bytes accessed | tf_op | source)
XLA Modules:
  0.0 51.9 jit_solution(14742424470242392652)
XLA Ops:
  0.6 49.2 %shard_map.95 = (bf16[32,4096]{1,0:T(8,128)(2,1)}, bf16[512,256]{1,0:T(8,128)(2,1)}) custom-call(s32[64]{0:T(128)} %order_h.1, f32[16]{0:T(128)} %band_gain_h.1, f32[32,32]{1,0:T(8,128)} %vroot_h.1, bf16[512,256]{1,0:T(8,128)(2,1)} %bitcast.4, s32[256]{0:T(256)} %band_h.1, bf16[32,4096]{1,0:T(8,128)(2,1)} %gradient_h.1, bf16[16,32,4096]{2,1,0:T(8,128)(2,1)} %anomalies.1, ...), custom_call_target="tpu_custom_call" | custom-call | tf_op jit(solution)/shard_map/pallas_call | solution.py:772
  49.8 2.0 %shard_map.96 = (f32[32,4096]{1,0:T(8,128)}, f32[512,256]{1,0:T(8,128)}) custom-call(bf16[32,4096]{1,0:T(8,128)(2,1)} %get-tuple-element.6.inc, bf16[512,256]{1,0:T(8,128)(2,1)} %get-tuple-element.7.grad), custom_call_target="tpu_custom_call" | custom-call | tf_op jit(solution)/shard_map/pallas_call | solution.py:788

commit v4 on v3

--- a/solution.py
+++ b/solution.py
@@ -426,10 +426,10 @@
     take_in = [ex.take_inner for ex in coef_ex] if line else []
     take_out = [ex.take_outer for ex in coef_ex] if line else []
     services = {
-        3: lambda: on_inner(take_in[0], gathers[0].start),
+        3: lambda: on_inner(take_in[0]),
         5: lambda: on_inner(take_in[1]),
         6: lambda: on_outer(take_out[0], gathers[0].start),
-        7: lambda: on_inner(take_in[2]),
+        7: lambda: on_inner(take_in[2], gathers[0].start),
     }
 
     def unit(n, carry):
@@ -476,10 +476,13 @@
     corner = pair_at([qpeer[3]]) if square else []
 
     def spread(c, blocks, start, last, hooks={}):
+        wide = 1 if last else 2
+        extent = wide * width
+
         def part(j, carry):
             for k, hook in hooks.items():
-                pl.when(j == k)(hook)
-            at = pl.ds(pl.multiple_of(j * width, width), width)
+                pl.when(j == k // wide)(hook)
+            at = pl.ds(pl.multiple_of(j * extent, extent), extent)
             field = product(c, blocks, at)
             if not start:
                 field = field + r.acc[c, :, at]
@@ -499,7 +502,7 @@
 
             return carry
 
-        lax.fori_loop(0, STRIPS, part, 0)
+        lax.fori_loop(0, STRIPS // wide, part, 0)
 
     def each(fn):
         def step(j, carry):
@@ -560,42 +563,43 @@
         scoped("combine", lambda: combine(jnp.int32(units - 1)))
         scoped("mate", gathers[0].mate.wait_recv, gathers[1].mate.wait_recv)
         scoped("home0", lambda: spread(0, of((0, 1), home), True, False, {
-            1: lambda: on_inner(take_in[3]),
-            2: go(lambda: on_outer(take_out[2]), gathers[2].start),
-            3: lambda: on_inner(gathers[3].start),
+            1: lambda: on_inner(take_in[3], gathers[2].start),
+            2: lambda: on_inner(gathers[3].start),
         }))
         scoped("adjoint0", lambda: adjoint(0))
+        scoped("start2", lambda: on_outer(take_out[2], gathers[2].start))
         scoped("adjoint1", lambda: adjoint(1))
         scoped("pass0", gathers[0].pass_on)
-        scoped("home1", gathers[2].mate.wait_recv, lambda: spread(1, of((0,), home), True, False))
+        scoped("home1", gathers[2].mate.wait_recv, lambda: spread(1, of((0,), home), True, False, {
+            2: lambda: on_outer(take_out[3], gathers[3].start),
+        }))
         scoped("fin0", gathers[0].finish)
         scoped("side0", lambda: spread(0, of((0,), sides), False, False, {
-            0: lambda: on_outer(take_out[3], gathers[3].start),
             1: gathers[1].pass_on,
         }))
-        scoped("far0", gathers[0].pass_far)
         scoped("fin1", gathers[1].finish)
         scoped("side1", lambda: spread(0, of((1,), sides), False, False, {
-            1: gathers[2].pass_on,
-            2: lambda: on_inner(grad_ex[0].relay),
+            0: gathers[0].pass_far,
+            1: lambda: on_inner(grad_ex[0].relay),
+            2: gathers[2].pass_on,
         }))
         scoped("home2", gathers[3].mate.wait_recv, lambda: spread(1, of((1,), home), False, False, {
             0: gathers[1].pass_far,
+            2: gathers[3].pass_on,
+            3: lambda: on_inner(grad_ex[1].relay),
         }))
         scoped("finf0", gathers[0].finish_far, gathers[1].finish_far)
         scoped("corner0", lambda: spread(0, of((0, 1), corner), False, True, {
-            1: gathers[3].pass_on,
-            2: lambda: on_inner(grad_ex[1].relay),
-            3: gathers[2].pass_far,
+            1: gathers[2].pass_far,
+            3: gathers[3].pass_far,
         }))
         scoped("fin23", gathers[2].finish, gathers[3].finish)
         scoped("side23", lambda: spread(1, of((0, 1), sides), False, False, {
-            2: lambda: grad_inner(0),
-            3: gathers[3].pass_far,
+            1: lambda: grad_inner(0),
+            3: lambda: inner_sum(0),
         }))
         scoped("finf1", gathers[2].finish_far, gathers[3].finish_far)
-        scoped("corner1", lambda: spread(1, of((0, 1), corner), False, True, {1: lambda: inner_sum(0)}))
-        scoped("grad1", lambda: grad_inner(1))
+        scoped("corner1", lambda: spread(1, of((0, 1), corner), False, True, {0: lambda: grad_inner(1)}))
         scoped("sum1", lambda: inner_sum(1))
         scoped("final0", lambda: inner_final(0))
         scoped("final1", lambda: inner_final(1))

time: 52.1 us -> 50.5 us (0.969)
  Pallas kernels: 51.2 us -> 49.7 us
    pallas_call x1, Pallas kernels: 49.2 us -> 47.6 us  [on_device(): pl.pallas_call(functools.partial(kernel, zn, sn, tuple(scratch)), out_sha...]
where the time goes in v4:
time: 50.5 us; the launch traced here: 50.3 us
  Pallas kernels  49.7 us (98%)
  between operations  0.64 us (1%)
    pallas_call x1, Pallas kernels, on_device(): pl.pallas_call(functools.partial(kernel, zn, sn, tuple(scratch)), out_sha...  47.6 us
    pallas_call x1, Pallas kernels, on_device(): pl.pallas_call(widen, out_shape=(jax.ShapeDtypeStruct((levels, columns),...  2.03 us

profile of v4, /device:TPU:0, one launch (start us, length us, event | category | flops | bytes accessed | tf_op | source)
XLA Modules:
  0.0 50.3 jit_solution(17464070358831070573)
XLA Ops:
  0.6 47.6 %shard_map.95 = (bf16[32,4096]{1,0:T(8,128)(2,1)}, bf16[512,256]{1,0:T(8,128)(2,1)}) custom-call(s32[64]{0:T(128)} %order_h.1, f32[16]{0:T(128)} %band_gain_h.1, f32[32,32]{1,0:T(8,128)} %vroot_h.1, bf16[512,256]{1,0:T(8,128)(2,1)} %bitcast.4, s32[256]{0:T(256)} %band_h.1, bf16[32,4096]{1,0:T(8,128)(2,1)} %gradient_h.1, bf16[16,32,4096]{2,1,0:T(8,128)(2,1)} %anomalies.1, ...), custom_call_target="tpu_custom_call" | custom-call | tf_op jit(solution)/shard_map/pallas_call | solution.py:776
  48.3 2.0 %shard_map.96 = (f32[32,4096]{1,0:T(8,128)}, f32[512,256]{1,0:T(8,128)}) custom-call(bf16[32,4096]{1,0:T(8,128)(2,1)} %get-tuple-element.6.inc, bf16[512,256]{1,0:T(8,128)(2,1)} %get-tuple-element.7.grad), custom_call_target="tpu_custom_call" | custom-call | tf_op jit(solution)/shard_map/pallas_call | solution.py:792

commit v5 on v4

--- a/solution.py
+++ b/solution.py
@@ -563,41 +563,26 @@
         scoped("combine", lambda: combine(jnp.int32(units - 1)))
         scoped("mate", gathers[0].mate.wait_recv, gathers[1].mate.wait_recv)
         scoped("home0", lambda: spread(0, of((0, 1), home), True, False, {
-            1: lambda: on_inner(take_in[3], gathers[2].start),
-            2: lambda: on_inner(gathers[3].start),
+            1: lambda: on_inner(take_in[3]),
         }))
         scoped("adjoint0", lambda: adjoint(0))
-        scoped("start2", lambda: on_outer(take_out[2], gathers[2].start))
+        scoped("start2", lambda: on_outer(take_out[2]), gathers[2].start)
         scoped("adjoint1", lambda: adjoint(1))
         scoped("pass0", gathers[0].pass_on)
         scoped("home1", gathers[2].mate.wait_recv, lambda: spread(1, of((0,), home), True, False, {
-            2: lambda: on_outer(take_out[3], gathers[3].start),
+            2: go(lambda: on_outer(take_out[3]), gathers[3].start),
         }))
         scoped("fin0", gathers[0].finish)
         scoped("side0", lambda: spread(0, of((0,), sides), False, False, {
             1: gathers[1].pass_on,
         }))
         scoped("fin1", gathers[1].finish)
-        scoped("side1", lambda: spread(0, of((1,), sides), False, False, {
-            0: gathers[0].pass_far,
-            1: lambda: on_inner(grad_ex[0].relay),
-            2: gathers[2].pass_on,
-        }))
-        scoped("home2", gathers[3].mate.wait_recv, lambda: spread(1, of((1,), home), False, False, {
-            0: gathers[1].pass_far,
-            2: gathers[3].pass_on,
-            3: lambda: on_inner(grad_ex[1].relay),
-        }))
+        scoped("side1", lambda: spread(0, of((1,), sides), False, False, {0: gathers[0].pass_far, 2: go(gathers[2].pass_on, lambda: on_inner(grad_ex[0].relay))}))
+        scoped("home2", gathers[3].mate.wait_recv, lambda: spread(1, of((1,), home), False, False, {0: gathers[1].pass_far, 2: gathers[3].pass_on}))
         scoped("finf0", gathers[0].finish_far, gathers[1].finish_far)
-        scoped("corner0", lambda: spread(0, of((0, 1), corner), False, True, {
-            1: gathers[2].pass_far,
-            3: gathers[3].pass_far,
-        }))
+        scoped("corner0", lambda: spread(0, of((0, 1), corner), False, True, {0: lambda: on_inner(grad_ex[1].relay), 3: gathers[2].pass_far}))
         scoped("fin23", gathers[2].finish, gathers[3].finish)
-        scoped("side23", lambda: spread(1, of((0, 1), sides), False, False, {
-            1: lambda: grad_inner(0),
-            3: lambda: inner_sum(0),
-        }))
+        scoped("side23", lambda: spread(1, of((0, 1), sides), False, False, {0: lambda: grad_inner(0), 2: go(gathers[3].pass_far, lambda: inner_sum(0))}))
         scoped("finf1", gathers[2].finish_far, gathers[3].finish_far)
         scoped("corner1", lambda: spread(1, of((0, 1), corner), False, True, {0: lambda: grad_inner(1)}))
         scoped("sum1", lambda: inner_sum(1))
@@ -638,19 +623,26 @@
         else:
             for ex in grad_ex:
                 ex.take()
-        for g in range(groups):
-            grad_out[:, g * gw : (g + 1) * gw] = r.got[g]
+        leaving = [
+            pltpu.make_async_copy(r.got.at[g], grad_out.at[:, pl.ds(g * gw, gw)], r.out_sem.at[g]) for g in range(groups)
+        ]
+        for copy in leaving:
+            copy.start()
 
     if line:
         with jax.named_scope("last"):
-            @pl.when(outer)
-            def _():
-                for c in range(HALVES):
+            for c in range(HALVES):
+
+                @pl.when(outer)
+                def _():
                     each(lambda j, c=c: final_of(c, j, near).wait_recv())
 
-            for c in range(HALVES):
                 for j in range(STRIPS):
-                    inc_out[c * lv : (c + 1) * lv, j * width : (j + 1) * width] = r.inc_all[c, j]
+                    at = (pl.ds(c * lv, lv), pl.ds(j * width, width))
+                    leaving.append(
+                        pltpu.make_async_copy(r.inc_all.at[c, j], inc_out.at[at], r.out_sem.at[groups + c * STRIPS + j])
+                    )
+                    leaving[-1].start()
 
         to(r.inc_sum, r.inc_got, r.inc_send.at[0], r.inc_recv.at[0, 0], mem=zpeer[1]).wait_send()
 
@@ -681,7 +673,9 @@
         for k in range(1, zn):
             held(k, zpeer[k]).wait_recv()
         for b in range(zn):
-            inc_out[:, b * strip : (b + 1) * strip] = r.inc_all[b]
+            at = (pl.ds(0, levels), pl.ds(b * strip, strip))
+            leaving.append(pltpu.make_async_copy(r.inc_all.at[b], inc_out.at[at], r.out_sem.at[groups + b]))
+            leaving[-1].start()
         for copy in sums + shares:
             copy.wait_send()
 
@@ -691,13 +685,30 @@
         for gather in gathers:
             gather.drain()
         to(r.pair_out, r.pair_in, r.pair_send, r.pair_recv.at[0], state=partner).wait_send()
+        for copy in leaving:
+            copy.wait()
         gone = r.rs_out.at[pl.ds(0, (qn - 1) * groups)]
         to(gone, gone, r.rs_send, r.rs_recv.at[0], state=partner).wait_send()
 
 
-def widen(inc, grad, inc_out, grad_out):
-    inc_out[...] = inc[...].astype(F32)
-    grad_out[...] = grad[...].astype(F32)
+def widen(inc, grad, inc_out, grad_out, inc_in, grad_in, inc_wide, grad_wide, arrive, leave):
+    jobs = []
+    for k, (src, held, wide, dst) in enumerate([(grad, grad_in, grad_wide, grad_out), (inc, inc_in, inc_wide, inc_out)]):
+        half = src.shape[0] // 2
+        for h in range(2):
+            at, n = pl.ds(h * half, half), 2 * k + h
+            jobs.append((
+                pltpu.make_async_copy(src.at[at], held.at[at], arrive.at[n]), held.at[at], wide.at[at],
+                pltpu.make_async_copy(wide.at[at], dst.at[at], leave.at[n]),
+            ))
+    for come, _, _, _ in jobs:
+        come.start()
+    for come, held, wide, go in jobs:
+        come.wait()
+        wide[...] = held[...].astype(F32)
+        go.start()
+    for _, _, _, go in jobs:
+        go.wait()
 
 
 def on_device(zn, sn, anomalies, alpha, basis, gradient, vertical_root, band_gain, band, order):
@@ -713,7 +724,6 @@
     arrivals = 2 if qn == 4 else qn - 1
     width = columns // STRIPS
     line = zn == 4
-    vmem = pl.BlockSpec(memory_space=pltpu.VMEM)
     hbm = pl.BlockSpec(memory_space=pl.ANY)
     dma = pltpu.SemaphoreType.DMA
     lookup = (1, -(-slots // LANES) * LANES)
@@ -742,6 +752,7 @@
         acc=pltpu.VMEM((HALVES, members * lv, columns), F32),
         inc_part=pltpu.VMEM((levels, columns), F32),
         load_sem=dma((7,)),
+        out_sem=dma((groups + max(zn, HALVES * STRIPS),)),
         band_gain=pltpu.SMEM(band_gain.shape, F32),
         order=pltpu.SMEM(order.shape, jnp.int32),
         base_sem=dma((groups * qn,)),
@@ -780,7 +791,7 @@
             jax.ShapeDtypeStruct((rows, modes), BF16),
         ),
         in_specs=[hbm] * 8,
-        out_specs=(vmem, vmem),
+        out_specs=(hbm, hbm),
         scratch_shapes=list(scratch.values()),
         compiler_params=pltpu.CompilerParams(
             collective_id=0, has_side_effects=True, vmem_limit_bytes=58 * 2**20
@@ -795,8 +806,16 @@
             jax.ShapeDtypeStruct((levels, columns), F32),
             jax.ShapeDtypeStruct((rows, modes), F32),
         ),
-        in_specs=[vmem] * 2,
-        out_specs=(vmem, vmem),
+        in_specs=[hbm] * 2,
+        out_specs=(hbm, hbm),
+        scratch_shapes=[
+            pltpu.VMEM((levels, columns), BF16),
+            pltpu.VMEM((rows, modes), BF16),
+            pltpu.VMEM((levels, columns), F32),
+            pltpu.VMEM((rows, modes), F32),
+            dma((4,)),
+            dma((4,)),
+        ],
     )(increment, grads)
     return increment, grads.reshape(members, levels, modes)
 

time: 50.5 us -> 50.2 us (level)
  no operation moved by 1% of the time
where the time goes in v5:
time: 50.2 us; the launch traced here: 49.9 us
  Pallas kernels  49.3 us (98%)
  between operations  0.64 us (1%)
    pallas_call x1, Pallas kernels, on_device(): pl.pallas_call(functools.partial(kernel, zn, sn, tuple(scratch)), out_sha...  47.4 us
    pallas_call x1, Pallas kernels, on_device(): pl.pallas_call(widen, out_shape=(jax.ShapeDtypeStruct((levels, columns),...  1.95 us

profile of v5, /device:TPU:0, one launch (start us, length us, event | category | flops | bytes accessed | tf_op | source)
XLA Modules:
  0.0 49.9 jit_solution(6517283443812968791)
XLA Ops:
  0.6 47.4 %shard_map.95 = (bf16[32,4096]{1,0:T(8,128)(2,1)}, bf16[512,256]{1,0:T(8,128)(2,1)}) custom-call(s32[64]{0:T(128)} %order_h.1, f32[16]{0:T(128)} %band_gain_h.1, f32[32,32]{1,0:T(8,128)} %vroot_h.1, bf16[512,256]{1,0:T(8,128)(2,1)} %bitcast.4, s32[256]{0:T(256)} %band_h.1, bf16[32,4096]{1,0:T(8,128)(2,1)} %gradient_h.1, bf16[16,32,4096]{2,1,0:T(8,128)(2,1)} %anomalies.1, ...), custom_call_target="tpu_custom_call" | custom-call | tf_op jit(solution)/shard_map/pallas_call | solution.py:787
  48.0 2.0 %shard_map.96 = (f32[32,4096]{1,0:T(8,128)}, f32[512,256]{1,0:T(8,128)}) custom-call(bf16[32,4096]{1,0:T(8,128)(2,1)} %get-tuple-element.6.inc, bf16[512,256]{1,0:T(8,128)(2,1)} %get-tuple-element.7.grad), custom_call_target="tpu_custom_call" | custom-call | tf_op jit(solution)/shard_map/pallas_call | solution.py:803
